TPU v7x, 32 devices: a whole 2x2x4 slice. The times are simulated.
32 devices in a mesh: gx: 4 (over z), gy: 4 (over y, core), gz: 2 (over x).
Axes of the slice: x: 2, y: 2, z: 4, core: 2. Of those that a mesh axis runs over, the one named last changes fastest.
Arguments:
- positions: float32 [8, 4, 16, 3, 128], P(('gx', 'gz'), 'gy'), may hold values from 0 to 1
- masses: float32 [8, 4, 16, 128], P(('gx', 'gz'), 'gy'), may hold values from 0.2 to 2
- velocities: float32 [8, 4, 16, 3, 128], P(('gx', 'gz'), 'gy'), may hold values from -6 to 6
- tile_counts: int32 [8, 4, 16], P(('gx', 'gz'), 'gy'), may hold values from 32 to 128
- neighbour_list: int32 [8, 4, 16, 6], P(('gx', 'gz'), 'gy'), may hold values from 0 to 143, as said below
Outputs:
- kicked: float32 [8, 4, 16, 3, 128], P(('gx', 'gz'), 'gy')
Inputs may be any that keep to these rules, and one draw needn't show every extreme that they name: `neighbour_list`: each entry is ((dx + 1) * 3 + dy + 1) * 16 + (t + dz) mod 16 for the tile t it belongs to, dx, dy, dz each in -1, 0, 1; the 6 entries of one tile name distinct shell tiles.
All inputs are finite; a program needn't handle non-finite values.
Results may differ from a plain program's by a relative error of at most 0.0003.
Values sent between devices are 32-bit elements; how exact they have to be, the bound alone decides.
A program may use at most 64 MiB of HBM per device.

v0:
```python
import functools
import math

import jax
import jax.numpy as jnp
import numpy as np
from jax import lax
from jax.experimental import pallas as pl
from jax.experimental.pallas import tpu as pltpu
from jax.sharding import PartitionSpec as P

CX = 2
CY = 6
NZ = 1024


smoothing = 0.1
screening = 0.01
split_scale = 2.0
softening = 0.05
long_kick = 1.0
short_kick = 0.05
highest = lax.Precision.HIGHEST


def padded(cells, sides, width):
    for axis, dim in sides:
        count = lax.axis_size(axis)
        head = lax.slice_in_dim(cells, 0, width, axis=dim)
        tail = lax.slice_in_dim(cells, cells.shape[dim] - width, cells.shape[dim], axis=dim)
        cells = jnp.concatenate(
            [
                lax.ppermute(tail, axis, [(i, (i + 1) % count) for i in range(count)]),
                cells,
                lax.ppermute(head, axis, [((i + 1) % count, i) for i in range(count)]),
            ],
            axis=dim,
        )
    return cells


def wave_terms(length, first_index, extent):
    wavenum = (first_index + jnp.arange(extent, dtype=jnp.int32)).astype(jnp.float32)
    angles = wavenum * (2.0 * jnp.pi / length)
    return (4.0 * jnp.sin(0.5 * angles) ** 2, jnp.sin(angles))


def cloud_stencil(positions, cells_x, cells_y, cells_z, tiles):
    span = cells_z // tiles
    tile_row = jnp.arange(tiles, dtype=jnp.int32)[:, None]
    coord_x = positions[..., 0, :] * cells_x - 0.5
    base_x = jnp.clip(jnp.floor(coord_x), 0, cells_x - 2)
    frac_x = jnp.clip(coord_x - base_x, 0.0, 1.0)
    coord_y = positions[..., 1, :] * cells_y - 0.5
    base_y = jnp.clip(jnp.floor(coord_y), 0, cells_y - 2)
    frac_y = jnp.clip(coord_y - base_y, 0.0, 1.0)
    coord_z = (tile_row + positions[..., 2, :]) * span - 0.5
    base_z = jnp.floor(coord_z)
    frac_z = coord_z - base_z
    index_x = base_x.astype(jnp.int32)
    index_y = base_y.astype(jnp.int32)
    index_z = base_z.astype(jnp.int32) % cells_z
    cell_list = []
    weight_list = []
    for offset_x in (0, 1):
        for offset_y in (0, 1):
            for offset_z in (0, 1):
                weight_x = frac_x if offset_x else 1.0 - frac_x
                weight_y = frac_y if offset_y else 1.0 - frac_y
                weight_z = frac_z if offset_z else 1.0 - frac_z
                cell_list.append(
                    ((index_x + offset_x) * cells_y + index_y + offset_y) * cells_z
                    + (index_z + offset_z) % cells_z
                )
                weight_list.append(weight_x * weight_y * weight_z)
    return (jnp.stack(cell_list, axis=-2), jnp.stack(weight_list, axis=-2))


def pair_accel(receivers, sources, shifts):
    parts = []
    for comp in range(3):
        parts.append(
            shifts[:, :, comp, None, None]
            + sources[:, :, comp, None, :]
            - receivers[:, None, comp, :, None]
        )
    square = parts[0] * parts[0] + parts[1] * parts[1] + parts[2] * parts[2]
    strength = (
        sources[:, :, 3, None, :] * jnp.exp(-square / split_scale) * (square + softening) ** (-1.5)
    )
    return jnp.stack([jnp.sum(strength * parts[comp], axis=(1, 3)) for comp in range(3)], axis=1)


def split_length(length):
    divisor = 1
    for factor in range(1, math.isqrt(length) + 1):
        if length % factor == 0:
            divisor = factor
    return divisor


def dft_table(length):
    indices = jnp.arange(length, dtype=jnp.int32)
    phases = indices[:, None] * indices[None, :] % length
    angles = phases.astype(jnp.float32) * (2.0 * jnp.pi / length)
    return (jnp.cos(angles), jnp.sin(angles))


def twiddle_table(outer, inner):
    length = outer * inner
    phases = (
        jnp.arange(outer, dtype=jnp.int32)[:, None]
        * jnp.arange(inner, dtype=jnp.int32)[None, :]
        % length
    )
    angles = phases.astype(jnp.float32) * (2.0 * jnp.pi / length)
    return (jnp.cos(angles), jnp.sin(angles))


def complex_mix(real, imag, cosine, sine_table, sign, form):
    real_cos = jnp.einsum(form, real, cosine, precision=highest)
    real_sin = jnp.einsum(form, real, sine_table, precision=highest)
    imag_cos = jnp.einsum(form, imag, cosine, precision=highest)
    imag_sin = jnp.einsum(form, imag, sine_table, precision=highest)
    return (real_cos - sign * imag_sin, imag_cos + sign * real_sin)


def transform_last(real, imag, sign):
    length = real.shape[-1]
    outer = split_length(length)
    inner = length // outer
    leading = real.shape[:-1]
    real = real.reshape(leading + (outer, inner))
    imag = imag.reshape(leading + (outer, inner))
    cos_outer, sin_outer = dft_table(outer)
    real, imag = complex_mix(real, imag, cos_outer, sin_outer, sign, "...pq,pk->...kq")
    turn_cos, turn_sin = twiddle_table(outer, inner)
    real, imag = (
        real * turn_cos - sign * imag * turn_sin,
        imag * turn_cos + sign * real * turn_sin,
    )
    cos_inner, sin_inner = dft_table(inner)
    real, imag = complex_mix(real, imag, cos_inner, sin_inner, sign, "...kq,qm->...mk")
    return (real.reshape(leading + (length,)), imag.reshape(leading + (length,)))


def transform_axis(fields, axis, sign):
    real = jnp.moveaxis(fields[:, 0], axis, -1)
    imag = jnp.moveaxis(fields[:, 1], axis, -1)
    real, imag = transform_last(real, imag, sign)
    return jnp.stack([jnp.moveaxis(real, -1, axis), jnp.moveaxis(imag, -1, axis)], axis=1)


def rotate(fields, factor):
    return jnp.stack([factor * fields[:, 1], -factor * fields[:, 0]], axis=1)


def shards(positions, masses, velocities, tile_counts, neighbour_list):
    tiles = positions.shape[2]
    listed = neighbour_list.shape[3]
    slot_index = jnp.arange(128, dtype=jnp.int32)
    live_mask = (slot_index < tile_counts[..., None]).astype(jnp.float32)
    mass_live = masses * live_mask
    packed = jnp.concatenate([positions, mass_live[:, :, :, None, :]], axis=3)
    shell = padded(packed, ((("gx", "gz"), 0), ("gy", 1)), 1)
    cell_index, cloud_weights = cloud_stencil(positions, CX, CY, NZ, tiles)
    amounts = cloud_weights * mass_live[:, :, :, None, :]
    density = jax.ops.segment_sum(
        amounts.reshape(-1), cell_index.reshape(-1), num_segments=CX * CY * NZ
    ).reshape(CX, CY, NZ)
    spectrum = jnp.stack([density, jnp.zeros_like(density)], axis=0)[None]
    spectrum = transform_axis(spectrum, 3, -1.0)
    spectrum = lax.all_to_all(spectrum, "gy", split_axis=4, concat_axis=3, tiled=True)
    span_y = spectrum.shape[3]
    spectrum = transform_axis(spectrum, 2, -1.0)
    spectrum = lax.all_to_all(spectrum, ("gx", "gz"), split_axis=3, concat_axis=2, tiled=True)
    span_x = spectrum.shape[2]
    spectrum = transform_axis(spectrum, 1, -1.0)
    block_y = spectrum.shape[3]
    block_z = spectrum.shape[4]
    kappa_x, sine_x = wave_terms(span_x, 0, span_x)
    kappa_y, sine_y = wave_terms(span_y, lax.axis_index(("gx", "gz")) * block_y, block_y)
    kappa_z, sine_z = wave_terms(NZ, lax.axis_index("gy") * block_z, block_z)
    kappa_sum = kappa_x[:, None, None] + kappa_y[None, :, None] + kappa_z[None, None, :]
    potential = spectrum * (-jnp.exp(-smoothing * kappa_sum) / (kappa_sum + screening))
    fields = jnp.concatenate([rotate(potential, sine_x[:, None, None]), potential], axis=0)
    fields = transform_axis(fields, 1, 1.0) / span_x
    fields = lax.all_to_all(fields, ("gx", "gz"), split_axis=2, concat_axis=3, tiled=True)
    whole_sine_y = wave_terms(span_y, 0, span_y)[1]
    fields = jnp.concatenate(
        [fields[0:1], rotate(fields[1:2], whole_sine_y[None, :, None]), fields[1:2]], axis=0
    )
    fields = transform_axis(fields, 2, 1.0) / span_y
    fields = lax.all_to_all(fields, "gy", split_axis=3, concat_axis=4, tiled=True)
    whole_sine_z = wave_terms(NZ, 0, NZ)[1]
    fields = jnp.concatenate(
        [fields[0:2], rotate(fields[2:3], whole_sine_z[None, None, :])], axis=0
    )
    fields = transform_axis(fields, 3, 1.0) / NZ
    forces = fields[:, 0]
    flat_forces = forces.reshape(3, -1)
    picked = flat_forces[:, cell_index]
    long_accel = jnp.moveaxis(jnp.sum(cloud_weights[None] * picked, axis=4), 0, 3)
    flat_shell = shell.reshape(9 * tiles, 4, 128)
    own_list = neighbour_list[0, 0]
    sources = flat_shell[own_list]
    groups = own_list // tiles
    layers = own_list % tiles
    tile_row = jnp.arange(tiles, dtype=jnp.int32)[:, None]
    shifts = jnp.stack(
        [groups // 3 - 1, groups % 3 - 1, (layers - tile_row + 1) % tiles - 1], axis=-1
    ).astype(jnp.float32)
    short_accel = lax.map(
        lambda pieces: pair_accel(*pieces),
        (
            positions[0, 0].reshape(tiles, 1, 3, 128),
            sources.reshape(tiles, 1, listed, 4, 128),
            shifts.reshape(tiles, 1, listed, 3),
        ),
    )
    short_accel = short_accel.reshape(1, 1, tiles, 3, 128)
    return velocities + live_mask[:, :, :, None, :] * (
        long_kick * long_accel + short_kick * short_accel
    )


MESH = pl.DeviceIdType.MESH
LOGICAL = pl.DeviceIdType.LOGICAL
f32 = jnp.float32
bf16 = jnp.bfloat16


def halves(x):
    high = x.astype(bf16)
    return high, (x - high.astype(f32)).astype(bf16)


def dot3(a, b, dims=((1,), (0,))):
    dot = functools.partial(
        lax.dot_general, dimension_numbers=(dims, ((), ())), preferred_element_type=f32
    )
    return dot(a[0], b[0]) + dot(a[1], b[0]) + dot(a[0], b[1])


def hat(coord, cell):
    return jnp.maximum(0.0, 1.0 - jnp.abs(coord - cell))


def np_halves(table):
    table = jnp.asarray(np.asarray(table, np.float32))
    return jnp.stack(halves(table))


def tables(size_x, size_y, size_z, tiles):
    rows, cols = size_x * size_z, size_y
    count = rows * cols
    modes = NZ // 2 // count
    pack = 128 // (2 * modes)
    span = NZ // tiles
    lane = np.arange(NZ)
    block, inside = lane // (2 * modes), lane % (2 * modes)
    imag = inside >= modes
    mode = block * modes + inside % modes
    nyquist = (mode == 0) & imag
    cells = np.arange(128) - 1
    angle = 2 * np.pi * ((cells[:, None] * mode[None, :]) % NZ) / NZ
    wave = np.where(imag[None], -np.sin(angle), np.cos(angle))
    wave = np.where(nyquist[None], np.cos(np.pi * (cells % 2))[:, None], wave)
    wave = np.where((cells <= span)[:, None], wave, 0.0)
    groups = NZ // 128
    forward = wave.reshape(128, groups, 128).transpose(1, 0, 2)
    scale = np.where(mode == 0, 1.0, 2.0) / (NZ * rows * CX * cols * CY)
    inverse = (wave * scale[None]).T
    turn = 2 * np.pi * ((mode[None] * np.arange(tiles)[:, None] * span) % NZ) / NZ
    cosine = np.cos(turn)
    sine = np.where(imag[None], 1.0, -1.0) * np.sin(turn)
    turns = np.stack([cosine, sine]).reshape(2, tiles, groups, 128)
    turns = turns.transpose(0, 2, 1, 3).reshape(2 * groups, tiles, 128)
    index = np.arange(3 * count * 4)
    device, row = index // 4 % count, index // (4 * count) * 4 + index % 4
    real = row < CX * CY
    place_x = device // (size_y * size_z) * size_z + device % size_z
    place_y = device // size_z % size_y
    nx, ny = rows * CX, cols * CY
    x = np.where(real, place_x * CX + row // CY, 0)
    y = np.where(real, place_y * CY + row % CY, 0)
    phase = (x[:, None] * x[None] * ny + y[:, None] * y[None] * nx) % (nx * ny)
    phase = 2 * np.pi * phase / (nx * ny)
    both = (real[:, None] & real[None]).astype(np.float64)
    plane = np.concatenate([np.cos(phase) * both, np.sin(phase) * both])
    lanes = np.zeros((8, 3 * count * 4))
    lanes[0] = 4 * np.sin(np.pi * x / nx) ** 2 + 4 * np.sin(np.pi * y / ny) ** 2
    lanes[1] = np.sin(2 * np.pi * x / nx)
    lanes[2] = np.sin(2 * np.pi * y / ny)
    return (
        np_halves(forward),
        np_halves(inverse),
        np_halves(plane),
        jnp.asarray(turns, f32),
        jnp.asarray(lanes, f32),
    )


def kick_kernel(
    sizes,
    pos_ref, mass_ref, vel_ref, turns_ref, lanes_ref, counts_ref, list_ref,
    forward_hbm, inverse_hbm, plane_hbm,
    out_ref,
    forward_ref, inverse_ref, plane_ref, shell_ref, rho_ref, spec_ref, got_ref,
    back_ref, home_ref, line_ref, swap_ref, field_ref, spread_ref, accum_ref, short_ref,
    table_sem, halo_send, halo_recv, out_send, out_recv, back_send, back_recv,
):
    size_x, size_y, size_z, tiles, listed = sizes
    rows, cols = size_x * size_z, size_y
    count = rows * cols
    modes = NZ // 2 // count
    width = 2 * modes
    pack = 128 // width
    groups = NZ // 128
    span = NZ // tiles
    gx, gy, gz = lax.axis_index("gx"), lax.axis_index("gy"), lax.axis_index("gz")
    row, col = gx * size_z + gz, gy
    me = (gx * size_y + gy) * size_z + gz

    def place(r, c):
        return (r // size_z, c, r % size_z)

    def other(i):
        d = me + i
        return jnp.where(d >= count, d - count, d)

    barrier = pltpu.get_barrier_semaphore()

    def greet(i, carry):
        pl.semaphore_signal(
            barrier, inc=1, device_id=other(i), device_id_type=LOGICAL
        )
        return carry

    lax.fori_loop(1, count, greet, 0)
    table_copies = [
        pltpu.make_async_copy(a, b, table_sem.at[i])
        for i, (a, b) in enumerate(
            ((forward_hbm, forward_ref), (plane_hbm, plane_ref), (inverse_hbm, inverse_ref))
        )
    ]
    for copy in table_copies:
        copy.start()

    slot = lax.broadcasted_iota(jnp.int32, (1, 128), 1)
    row_of = lax.broadcasted_iota(jnp.int32, (16, 128), 0)
    cell_x = (row_of // CY).astype(f32)
    cell_y = (row_of % CY).astype(f32)
    cell_z = lax.broadcasted_iota(jnp.int32, (128, 128), 0).astype(f32) - 1.0

    def weights(t):
        spot = [pos_ref[comp, pl.ds(t, 1), :] for comp in range(3)]
        coord_x = jnp.clip(spot[0] * CX - 0.5, 0.0, CX - 1.0)
        coord_y = jnp.clip(spot[1] * CY - 0.5, 0.0, CY - 1.0)
        start = jnp.asarray(t, jnp.int32).astype(f32)
        coord_z = (start + spot[2]) * span - 0.5 - start * span
        plane = hat(coord_x, cell_x) * hat(coord_y, cell_y)
        return plane, hat(coord_z, cell_z)

    own = 4 * tiles

    def gather(t, carry):
        live = (slot < counts_ref[t]).astype(f32)
        for comp in range(3):
            shell_ref[own + t, comp:comp + 1, :] = pos_ref[comp, pl.ds(t, 1), :]
        shell_ref[own + t, 3:4, :] = mass_ref[pl.ds(t, 1), :] * live
        return carry

    lax.fori_loop(0, tiles, gather, 0, unroll=4)
    def deposit(t, carry):
        mass = shell_ref[own + t, 3:4, :]
        plane, wz = weights(t)
        rho_ref[pl.ds(pl.multiple_of(t * 16, 16), 16), :] = dot3(
            halves(plane * mass), halves(wz), ((1,), (1,))
        )
        return carry

    lax.fori_loop(0, tiles, deposit, 0, unroll=4)
    def swapped(x):
        lane = lax.broadcasted_iota(jnp.int32, x.shape, 1)
        return jnp.where(
            (lane % width) < modes, pltpu.roll(x, 128 - modes, 1), pltpu.roll(x, modes, 1)
        )

    quarter = lax.broadcasted_iota(jnp.int32, (8, 128), 1) // width

    table_copies[0].wait()
    rho = halves(rho_ref[...])

    def transform(g, carry):
        wide = dot3(rho, (forward_ref[0, g], forward_ref[1, g]))
        cosine, sine = turns_ref[g], turns_ref[groups + g]
        straight = jnp.zeros((16, 128), f32)
        crossed = jnp.zeros((16, 128), f32)
        for t in range(tiles):
            part = wide[t * 16:(t + 1) * 16]
            straight = straight + part * cosine[t:t + 1]
            crossed = crossed + part * sine[t:t + 1]
        lines = straight + swapped(crossed)
        thirds = (lines[0:8], pltpu.roll(lines[0:8], 4, 0), lines[8:16])
        for i in range(pack):
            packed = jnp.zeros((8, 128), f32)
            for a, third in enumerate(thirds):
                shift = (a - i) * width % 128
                piece = pltpu.roll(third, shift, 1) if shift else third
                packed = jnp.where(quarter == a, piece, packed)
            spec_ref[g * pack + i] = packed[0:4]
        return carry

    lax.fori_loop(0, groups, transform, 0)

    def out_copy(d):
        return pltpu.make_async_remote_copy(
            src_ref=spec_ref.at[d],
            dst_ref=got_ref.at[me],
            send_sem=out_send,
            recv_sem=out_recv,
            device_id=d,
            device_id_type=LOGICAL,
        )

    def back_copy(d):
        return pltpu.make_async_remote_copy(
            src_ref=back_ref.at[d],
            dst_ref=home_ref.at[me],
            send_sem=back_send,
            recv_sem=back_recv,
            device_id=d,
            device_id_type=LOGICAL,
        )

    def start_all(make):
        def step(i, carry):
            make(other(i)).start()
            return carry

        lax.fori_loop(1, count, step, 0)

    def wait_all(ref, sem):
        rest = ref.at[pl.ds(0, count - 1)]
        pltpu.make_async_copy(rest, rest, sem).wait()

    pl.semaphore_wait(barrier, count - 1)
    start_all(out_copy)
    halos = []
    for step_x in (-1, 0, 1):
        for step_y in (-1, 0, 1):
            if step_x == 0 and step_y == 0:
                continue
            slot_there = (1 - step_x) * 3 + 1 - step_y
            halos.append(
                pltpu.make_async_remote_copy(
                    src_ref=shell_ref.at[pl.ds(own, tiles)],
                    dst_ref=shell_ref.at[pl.ds(slot_there * tiles, tiles)],
                    send_sem=halo_send.at[slot_there],
                    recv_sem=halo_recv.at[slot_there],
                    device_id=place((row + step_x + rows) % rows, (col + step_y + cols) % cols),
                    device_id_type=MESH,
                )
            )
    for copy in halos:
        copy.start()
    got_ref[me] = spec_ref[me]

    ones = jnp.ones((8, 128), bf16)
    block = 32

    def spread(t, carry):
        for comp in range(3):
            spread_ref[t, comp] = jnp.transpose(
                jnp.broadcast_to(pos_ref[comp, pl.ds(t, 1), :], (128, 128)), (1, 0)
            )
        return carry

    lax.fori_loop(0, tiles, spread, 0)

    def pairs(t, carry):
        sources = []
        for n in range(listed):
            entry = list_ref[n, 0, t]
            group, layer = entry // tiles, entry % tiles
            away = (layer - t + 1 + tiles) % tiles - 1
            tile = shell_ref[entry]
            sources.append(
                (
                    tile[0:1] + (group // 3 - 1).astype(f32),
                    tile[1:2] + (group % 3 - 1).astype(f32),
                    tile[2:3] + away.astype(f32),
                    tile[3:4],
                )
            )
        for b in range(128 // block):
            here = [spread_ref[t, comp, b * block:(b + 1) * block, :] for comp in range(3)]
            totals = [jnp.zeros((block, 128), f32) for comp in range(3)]
            for source in sources:
                parts = [source[comp] - here[comp] for comp in range(3)]
                square = parts[0] * parts[0] + parts[1] * parts[1] + parts[2] * parts[2]
                root = lax.rsqrt(square + softening)
                strength = source[3] * jnp.exp2(square * (-1.0 / (split_scale * math.log(2.0)))) * (root * root * root)
                totals = [totals[comp] + strength * parts[comp] for comp in range(3)]
            for comp in range(3):
                accum_ref[comp * 128 + b * block:comp * 128 + (b + 1) * block, :] = totals[comp]
        high, low = halves(accum_ref[...])
        dot = functools.partial(
            lax.dot_general,
            dimension_numbers=(((1,), (1,)), ((), ())),
            preferred_element_type=f32,
        )
        sums = dot(ones, high) + dot(ones, low)
        for comp in range(3):
            short_ref[comp, pl.ds(t, 1), :] = sums[0:1, comp * 128:(comp + 1) * 128]
        return carry

    depth = 3 * count * 4
    mode_of = lax.broadcasted_iota(jnp.int32, (modes, depth), 0) + me * modes
    packed = mode_of == 0
    keep = jnp.where(packed, 0.0, 1.0)
    kappa_xy, sine_x, sine_y = (lanes_ref[i:i + 1, :] for i in range(3))

    def green(which):
        kappa = kappa_xy + 4.0 * jnp.sin(which.astype(f32) * (jnp.pi / NZ)) ** 2
        return -jnp.exp(-smoothing * kappa) / (kappa + screening)

    g1 = green(mode_of)
    g2 = green(jnp.where(packed, NZ // 2, mode_of))
    sine_z = jnp.sin(mode_of.astype(f32) * (2.0 * jnp.pi / NZ))
    sine_z = jnp.concatenate([sine_z, sine_z], axis=0)
    wait_all(got_ref, out_recv)
    table_copies[1].wait()
    turned = jnp.transpose(got_ref[...].reshape(count * 4, 128), (1, 0))
    mine = halves(
        jnp.concatenate([turned[a * width:(a + 1) * width] for a in range(3)], axis=1)
    )
    by_cos = dot3(mine, (plane_ref[0, :depth], plane_ref[1, :depth]))
    by_sin = dot3(mine, (plane_ref[0, depth:], plane_ref[1, depth:]))
    cr, ci = by_cos[:modes], by_cos[modes:]
    sr, si = by_sin[:modes], by_sin[modes:]
    for_cos = jnp.concatenate([g1 * (keep * ci - sr), -g2 * (keep * cr + si)], axis=0)
    for_sin = jnp.concatenate([g1 * (cr + keep * si), g2 * (ci - keep * sr)], axis=0)
    stacked_cos = jnp.concatenate([for_cos * sine_x, for_cos * sine_y, for_cos * sine_z], axis=0)
    stacked_sin = jnp.concatenate([for_sin * sine_x, for_sin * sine_y, for_sin * sine_z], axis=0)
    result = dot3(halves(stacked_cos), (plane_ref[0, :depth], plane_ref[1, :depth])) + dot3(
        halves(stacked_sin), (plane_ref[0, depth:], plane_ref[1, depth:])
    )
    result = jnp.concatenate([result, jnp.zeros((128 - 3 * width, depth), f32)], axis=0)
    for a in range(3):
        third = jnp.transpose(result[:, a * count * 4:(a + 1) * count * 4], (1, 0))
        back_ref[:, a] = third.reshape(count, 4, 128)
    start_all(back_copy)
    home_ref[me] = back_ref[me]

    for copy in halos:
        copy.wait_recv()
    lax.fori_loop(0, tiles, pairs, 0, unroll=2)
    wait_all(home_ref, back_recv)
    table_copies[2].wait()

    near = quarter[0:4]
    for g in range(groups):
        for a in range(3):
            blocks = [home_ref[g * pack + i, a] for i in range(pack)]
            for f in range(3):
                merged = jnp.zeros((4, 128), f32)
                for i in range(pack):
                    shift = ((i - f) * width) % 128
                    piece = pltpu.roll(blocks[i], shift, 1) if shift else blocks[i]
                    merged = jnp.where(near == i, piece, merged)
                line_ref[g, f * 16 + a * 4:f * 16 + (a + 1) * 4, :] = merged
        for f in range(3):
            line_ref[g, f * 16 + 12:(f + 1) * 16, :] = jnp.zeros((4, 128), f32)
        swap_ref[g] = swapped(line_ref[g])

    together = 4

    def invert(q, carry):
        pieces = []
        total = jnp.zeros((together * 48, 128), f32)
        for g in range(groups):
            line, swap = line_ref[g], swap_ref[g]
            turned = []
            for i in range(together):
                t = q * together + i
                turned.append(
                    line * turns_ref[g, pl.ds(t, 1), :]
                    + swap * turns_ref[groups + g, pl.ds(t, 1), :]
                )
            part = halves(jnp.concatenate(turned, axis=0))
            at = slice(g * 128, (g + 1) * 128)
            total = total + dot3(part, (inverse_ref[0, at], inverse_ref[1, at]))
        field_ref[pl.ds(q * together, together)] = total.reshape(together, 48, 128)
        return carry

    lax.fori_loop(0, tiles // together, invert, 0)

    def interpolate(t, carry):
        plane, wz = weights(t)
        here = dot3(halves(field_ref[t]), halves(wz))
        live = (slot < counts_ref[t]).astype(f32)
        for f in range(3):
            pull = jnp.sum(here[f * 16:(f + 1) * 16] * plane, axis=0, keepdims=True)
            at = (f, pl.ds(t, 1), slice(None))
            out_ref[at] = vel_ref[at] + live * (long_kick * pull + short_kick * short_ref[at])
        return carry

    lax.fori_loop(0, tiles, interpolate, 0, unroll=4)
    for copy in halos:
        copy.wait_send()
    wait_all(got_ref, out_send)
    wait_all(home_ref, back_send)


def fused_shards(sizes, positions, masses, velocities, tile_counts, neighbour_list):
    size_x, size_y, size_z, tiles, listed = sizes
    rows, cols = size_x * size_z, size_y
    count = rows * cols
    groups = NZ // 128
    with jax.ensure_compile_time_eval():
        forward, inverse, plane, turns, lanes = tables(size_x, size_y, size_z, tiles)
    vmem = pl.BlockSpec(memory_space=pltpu.VMEM)
    smem = pl.BlockSpec(memory_space=pltpu.SMEM)
    anywhere = pl.BlockSpec(memory_space=pl.ANY)
    dma = pltpu.SemaphoreType.DMA
    kicked = pl.pallas_call(
        functools.partial(kick_kernel, sizes),
        out_shape=jax.ShapeDtypeStruct((3, tiles, 128), f32),
        in_specs=[vmem] * 5 + [smem] * 2 + [anywhere] * 3,
        out_specs=vmem,
        scratch_shapes=[
            pltpu.VMEM(forward.shape, bf16),
            pltpu.VMEM(inverse.shape, bf16),
            pltpu.VMEM(plane.shape, bf16),
            pltpu.VMEM((9 * tiles, 4, 128), f32),
            pltpu.VMEM((tiles * 16, 128), f32),
            pltpu.VMEM((count, 4, 128), f32),
            pltpu.VMEM((count, 4, 128), f32),
            pltpu.VMEM((count, 3, 4, 128), f32),
            pltpu.VMEM((count, 3, 4, 128), f32),
            pltpu.VMEM((groups, 48, 128), f32),
            pltpu.VMEM((groups, 48, 128), f32),
            pltpu.VMEM((tiles, 48, 128), f32),
            pltpu.VMEM((tiles, 3, 128, 128), f32),
            pltpu.VMEM((384, 128), f32),
            pltpu.VMEM((3, tiles, 128), f32),
            dma((3,)),
            dma((9,)),
            dma((9,)),
            dma,
            dma,
            dma,
            dma,
        ],
        compiler_params=pltpu.CompilerParams(collective_id=0, has_side_effects=True),
        name="kick",
    )(
        jnp.transpose(positions[0, 0], (1, 0, 2)),
        masses.reshape(tiles, 128),
        jnp.transpose(velocities[0, 0], (1, 0, 2)),
        turns,
        lanes,
        tile_counts.reshape(tiles),
        jnp.transpose(neighbour_list[0], (2, 0, 1)),
        forward,
        inverse,
        plane,
    )
    return jnp.transpose(kicked, (1, 0, 2))[None, None]


def fits(sizes):
    size_x, size_y, size_z, tiles, listed = sizes
    count = size_x * size_y * size_z
    if (NZ // 2) % count or count * 4 % 128 or CX * CY > 12 or count > 64:
        return False
    modes = NZ // 2 // count
    return modes == 16 and tiles % 4 == 0


def solution(mesh):
    placed = (
        P(("gx", "gz"), "gy", None, None, None),
        P(("gx", "gz"), "gy", None, None),
        P(("gx", "gz"), "gy", None, None, None),
        P(("gx", "gz"), "gy", None),
        P(("gx", "gz"), "gy", None, None),
    )

    def local(positions, masses, velocities, tile_counts, neighbour_list):
        sizes = tuple(mesh.shape[axis] for axis in ("gx", "gy", "gz"))
        sizes = sizes + (positions.shape[2], neighbour_list.shape[3])
        part = functools.partial(fused_shards, sizes) if fits(sizes) else shards
        return part(positions, masses, velocities, tile_counts, neighbour_list)

    return jax.shard_map(
        local,
        mesh=mesh,
        in_specs=placed,
        out_specs=P(("gx", "gz"), "gy", None, None, None),
        check_vma=False,
    )
```

profile of v0, /device:TPU:0, one launch (start us, length us, event | category | flops | bytes accessed | tf_op | source)
XLA Modules:
  0.0 27.8 jit_solution(7220421673606655005)
XLA Ops:
  0.0 26.5 %kick.1 = f32[3,16,128]{2,1,0:T(8,128)} custom-call(f32[3,16,128]{2,1,0:T(8,128)} %bitcast.15, f32[16,128]{1,0:T(8,128)} %bitcast.17, f32[3,16,128]{2,1,0:T(8,128)} %bitcast.16, f32[16,16,128]{2,1,0:T(8,128)} %constant.10.clone.turns_ref, f32[8,384]{1,0:T(8,128)} %constant.11.clone.lanes_ref, s32[16]{0:T(128)} %bitcast.19, s32[6,1,16]{2,1,0:T(1,128)} %bitcast.18, ...), custom_call_target="tpu_custom_call" | custom-call | tf_op jit(solution)/shard_map/kick/pallas_call | solution.py:628
  26.5 1.3 %copy.12 = f32[1,1,16,3,128]{4,2,3,1,0:T(8,128)} copy(f32[1,1,16,3,128]{4,2,3,1,0:T(8,128)} %bitcast.14) | data formatting | bytes 49152
where the time goes:
time: 28 us; the launch traced here: 27.8 us
  Pallas kernels  26.5 us (95%)
  local copies, waits for them, and re-layouts  1.35 us (5%)
    pallas_call x1, Pallas kernels, fused_shards(): pl.pallas_call(functools.partial(kick_kernel, sizes), out_shape=jax.Shape...  26.5 us
    unnamed x1, local copies, waits for them, and re-layouts  1.35 us

commit v1 on v0

--- a/solution.py
+++ b/solution.py
@@ -627,7 +627,7 @@
     dma = pltpu.SemaphoreType.DMA
     kicked = pl.pallas_call(
         functools.partial(kick_kernel, sizes),
-        out_shape=jax.ShapeDtypeStruct((3, tiles, 128), f32),
+        out_shape=pltpu.VMEM((3, tiles, 128), f32),
         in_specs=[vmem] * 5 + [smem] * 2 + [anywhere] * 3,
         out_specs=vmem,
         scratch_shapes=[

time: 28 us -> 26.7 us (0.954)
  local copies, waits for them, and re-layouts: 1.35 us -> 0.61 us
  Pallas kernels: 26.5 us -> 25.9 us
    unnamed x1, local copies, waits for them, and re-layouts: 1.35 us -> 0.61 us
    pallas_call x1, Pallas kernels: 26.5 us -> 25.9 us  [fused_shards(): pl.pallas_call(functools.partial(kick_kernel, sizes), out_shape=pltpu.VME...]
where the time goes in v1:
time: 26.7 us; the launch traced here: 26.5 us
  Pallas kernels  25.9 us (97%)
  local copies, waits for them, and re-layouts  0.61 us (2%)
    pallas_call x1, Pallas kernels, fused_shards(): pl.pallas_call(functools.partial(kick_kernel, sizes), out_shape=pltpu.VME...  25.9 us
    unnamed x1, local copies, waits for them, and re-layouts  0.61 us

profile of v1, /device:TPU:0, one launch (start us, length us, event | category | flops | bytes accessed | tf_op | source)
XLA Modules:
  0.0 26.5 jit_solution(313926621801200294)
XLA Ops:
  0.0 25.9 %kick.1 = f32[3,16,128]{2,1,0:T(8,128)S(1)} custom-call(f32[3,16,128]{2,1,0:T(8,128)} %bitcast.15, f32[16,128]{1,0:T(8,128)} %bitcast.17, f32[3,16,128]{2,1,0:T(8,128)} %bitcast.16, f32[16,16,128]{2,1,0:T(8,128)} %constant.10.clone.turns_ref, f32[8,384]{1,0:T(8,128)} %constant.11.clone.lanes_ref, s32[16]{0:T(128)} %bitcast.19, s32[6,1,16]{2,1,0:T(1,128)} %bitcast.18, ...), custom_call_target="tpu_custom_call" | custom-call | tf_op jit(solution)/shard_map/kick/pallas_call | solution.py:628
  25.9 0.6 %copy.12 = f32[1,1,16,3,128]{4,2,3,1,0:T(8,128)} copy(f32[1,1,16,3,128]{4,2,3,1,0:T(8,128)S(1)} %bitcast.14) | data formatting | bytes 49152

commit v2 on v1

--- a/solution.py
+++ b/solution.py
@@ -1,3 +1,4 @@
+import contextlib
 import functools
 import math
 
@@ -242,6 +243,10 @@
     return dot(a[0], b[0]) + dot(a[1], b[0]) + dot(a[0], b[1])
 
 
+def scope(name):
+    return contextlib.nullcontext()
+
+
 def hat(coord, cell):
     return jnp.maximum(0.0, 1.0 - jnp.abs(coord - cell))
 
@@ -249,6 +254,15 @@
 def np_halves(table):
     table = jnp.asarray(np.asarray(table, np.float32))
     return jnp.stack(halves(table))
+
+
+def stacked_dot(high, low, table_high, table_low, dims=((1,), (0,))):
+    dot = functools.partial(
+        lax.dot_general, dimension_numbers=(dims, ((), ())), preferred_element_type=f32
+    )
+    rows = high.shape[0]
+    both = dot(jnp.concatenate([high, low], axis=0), table_high)
+    return both[:rows] + both[rows:] + dot(high, table_low)
 
 
 def tables(size_x, size_y, size_z, tiles):
@@ -256,59 +270,102 @@
     count = rows * cols
     modes = NZ // 2 // count
     pack = 128 // (2 * modes)
-    span = NZ // tiles
-    lane = np.arange(NZ)
-    block, inside = lane // (2 * modes), lane % (2 * modes)
-    imag = inside >= modes
-    mode = block * modes + inside % modes
-    nyquist = (mode == 0) & imag
+    groups = tiles // 2
+    lane = np.arange(128)
+    member, imag, slot = lane // (2 * modes), lane % (2 * modes) >= modes, lane % modes
     cells = np.arange(128) - 1
-    angle = 2 * np.pi * ((cells[:, None] * mode[None, :]) % NZ) / NZ
-    wave = np.where(imag[None], -np.sin(angle), np.cos(angle))
-    wave = np.where(nyquist[None], np.cos(np.pi * (cells % 2))[:, None], wave)
-    wave = np.where((cells <= span)[:, None], wave, 0.0)
-    groups = NZ // 128
-    forward = wave.reshape(128, groups, 128).transpose(1, 0, 2)
-    scale = np.where(mode == 0, 1.0, 2.0) / (NZ * rows * CX * cols * CY)
-    inverse = (wave * scale[None]).T
-    turn = 2 * np.pi * ((mode[None] * np.arange(tiles)[:, None] * span) % NZ) / NZ
-    cosine = np.cos(turn)
-    sine = np.where(imag[None], 1.0, -1.0) * np.sin(turn)
-    turns = np.stack([cosine, sine]).reshape(2, tiles, groups, 128)
-    turns = turns.transpose(0, 2, 1, 3).reshape(2 * groups, tiles, 128)
-    index = np.arange(3 * count * 4)
-    device, row = index // 4 % count, index // (4 * count) * 4 + index % 4
-    real = row < CX * CY
+    cells[127] = -2
+    used = cells <= NZ // tiles + 1
+    waves = []
+    for g in range(groups):
+        plus = member < pack // 2
+        residue = np.where(plus, g, tiles - g if g else tiles // 2)
+        mode = tiles * (member % (pack // 2) * modes + slot) + residue
+        angle = 2 * np.pi * ((cells[:, None] * mode[None]) % NZ) / NZ
+        direct = np.where(imag[None], -np.sin(angle), np.cos(angle))
+        crossed = np.where(imag[None], np.cos(angle), np.sin(angle))
+        crossed = np.where(plus[None], -crossed, crossed)
+        if g == 0:
+            nyquist = (mode == 0) & imag
+            direct = np.where(nyquist[None], np.cos(np.pi * (cells % 2))[:, None], direct)
+            direct, crossed = (
+                np.where(plus[None], direct, 0.0),
+                np.where(plus[None], 0.0, direct),
+            )
+        both = np.stack([direct, crossed])
+        waves.append(np.where(used[None, :, None], both, 0.0).reshape(256, 128))
+    nx, ny = rows * CX, cols * CY
+    index = np.arange(4 * count * 4)
+    device, row = index // 4 % count, index // (4 * count) * (CX * CY // 4) + index % 4
+    real = index % 4 < CX * CY // 4
     place_x = device // (size_y * size_z) * size_z + device % size_z
     place_y = device // size_z % size_y
-    nx, ny = rows * CX, cols * CY
-    x = np.where(real, place_x * CX + row // CY, 0)
-    y = np.where(real, place_y * CY + row % CY, 0)
-    phase = (x[:, None] * x[None] * ny + y[:, None] * y[None] * nx) % (nx * ny)
-    phase = 2 * np.pi * phase / (nx * ny)
-    both = (real[:, None] & real[None]).astype(np.float64)
-    plane = np.concatenate([np.cos(phase) * both, np.sin(phase) * both])
-    lanes = np.zeros((8, 3 * count * 4))
-    lanes[0] = 4 * np.sin(np.pi * x / nx) ** 2 + 4 * np.sin(np.pi * y / ny) ** 2
-    lanes[1] = np.sin(2 * np.pi * x / nx)
-    lanes[2] = np.sin(2 * np.pi * y / ny)
-    return (
-        np_halves(forward),
-        np_halves(inverse),
-        np_halves(plane),
-        jnp.asarray(turns, f32),
-        jnp.asarray(lanes, f32),
-    )
+    here_x = np.where(real, place_x * CX + row // CY, 0)
+    here_y = np.where(real, place_y * CY + row % CY, 0)
+    wave_x, wave_y = np.arange(nx * ny) // ny, np.arange(nx * ny) % ny
+
+    def cas(x, y):
+        ax = 2 * np.pi * (x[:, None] * wave_x[None] % nx) / nx
+        ay = 2 * np.pi * (y[:, None] * wave_y[None] % ny) / ny
+        return (np.cos(ax) + np.sin(ax)) * (np.cos(ay) + np.sin(ay))
+
+    into = cas(here_x, here_y) * real[:, None]
+    outof = cas(wave_x, wave_y)
+    lanes = np.zeros((8, nx * ny))
+    lanes[:] = 4 * np.sin(np.pi * wave_x / nx) ** 2 + 4 * np.sin(np.pi * wave_y / ny) ** 2
+    return np_halves(np.stack(waves)), np_halves(into), np_halves(outof), jnp.asarray(lanes, f32)
+
+
+def tile_waves(even, odd):
+    half = len(even) - 1
+    ring, quarter = 2 * half, half // 2
+
+    def total(terms):
+        result = None
+        for factor, value in terms:
+            if abs(factor) < 1e-12:
+                continue
+            if abs(abs(factor) - 1.0) < 1e-12:
+                if result is None:
+                    result = value if factor > 0 else -value
+                else:
+                    result = result + value if factor > 0 else result - value
+            else:
+                part = value * float(abs(factor))
+                if result is None:
+                    result = part if factor > 0 else -part
+                else:
+                    result = result + part if factor > 0 else result - part
+        return result
+
+    sums = [even[t] + even[half - t] for t in range(quarter)]
+    gaps = [even[t] - even[half - t] for t in range(quarter)]
+    odd_sums = {t: odd[t] + odd[half - t] for t in range(1, quarter)}
+    odd_gaps = {t: odd[t] - odd[half - t] for t in range(1, quarter)}
+    cosines, sines = [], {}
+    for r in range(half + 1):
+        cos = [math.cos(2 * math.pi * r * t / ring) for t in range(quarter + 1)]
+        sin = [math.sin(2 * math.pi * r * t / ring) for t in range(quarter + 1)]
+        terms = [(cos[t], (gaps if r % 2 else sums)[t]) for t in range(quarter)]
+        if r % 2 == 0:
+            terms.append((cos[quarter], even[quarter]))
+        cosines.append(total(terms))
+        if 0 < r < half:
+            terms = [(sin[t], (odd_sums if r % 2 else odd_gaps)[t]) for t in range(1, quarter)]
+            if r % 2:
+                terms.append((sin[quarter], odd[quarter]))
+            sines[r] = total(terms)
+    return cosines, sines
 
 
 def kick_kernel(
     sizes,
-    pos_ref, mass_ref, vel_ref, turns_ref, lanes_ref, counts_ref, list_ref,
-    forward_hbm, inverse_hbm, plane_hbm,
+    pos_hbm, mass_hbm, vel_hbm, lanes_hbm, counts_hbm, list_hbm, wave_hbm, into_hbm, outof_hbm,
     out_ref,
-    forward_ref, inverse_ref, plane_ref, shell_ref, rho_ref, spec_ref, got_ref,
-    back_ref, home_ref, line_ref, swap_ref, field_ref, spread_ref, accum_ref, short_ref,
-    table_sem, halo_send, halo_recv, out_send, out_recv, back_send, back_recv,
+    pos_ref, mass_ref, vel_ref, lanes_ref, counts_ref, list_ref, wave_ref, into_ref, outof_ref,
+    shell_ref, rho_ref, weight_ref, spec_ref, got_ref, window_ref,
+    back_ref, home_ref, part_ref, field_ref, spread_ref, accum_ref, short_ref,
+    input_sem, halo_send, halo_recv, out_send, out_recv, back_send, back_recv,
 ):
     size_x, size_y, size_z, tiles, listed = sizes
     rows, cols = size_x * size_z, size_y
@@ -316,19 +373,53 @@
     modes = NZ // 2 // count
     width = 2 * modes
     pack = 128 // width
-    groups = NZ // 128
+    groups = tiles // 2
     span = NZ // tiles
+    near_cells = -(-(span + 3) // 16) * 16
+    share = CX * CY // 4
+    flat = size_y * size_z
     gx, gy, gz = lax.axis_index("gx"), lax.axis_index("gy"), lax.axis_index("gz")
     row, col = gx * size_z + gz, gy
     me = (gx * size_y + gy) * size_z + gz
 
+    copies = [
+        pltpu.make_async_copy(a, b, input_sem.at[i])
+        for i, (a, b) in enumerate(
+            (
+                (pos_hbm, pos_ref),
+                (mass_hbm, mass_ref),
+                (counts_hbm, counts_ref),
+                (wave_hbm, wave_ref),
+                (list_hbm, list_ref),
+                (lanes_hbm, lanes_ref),
+                (into_hbm, into_ref),
+                (outof_hbm, outof_ref),
+                (vel_hbm, vel_ref),
+            )
+        )
+    ]
+    for copy in copies[:3]:
+        copy.start()
+
     def place(r, c):
         return (r // size_z, c, r % size_z)
 
+    first = size_x - 1 - gx
+    second = lax.rem(gx + size_x // 2, size_x)
+    third = size_x - 1 - second
+    spot_here = gy * size_z + gz
+
     def other(i):
-        d = me + i
-        return jnp.where(d >= count, d - count, d)
-
+        if size_x != 4:
+            return lax.rem(me + 1 + i, count)
+        block = i // flat
+        away = lax.rem(i, flat) + jnp.where(block == 3, 1, 0)
+        plane = jnp.where(
+            block == 0, first, jnp.where(block == 1, second, jnp.where(block == 2, third, gx))
+        )
+        return plane * flat + lax.rem(spot_here + away, flat)
+
+    got_ref[...] = jnp.zeros((count, 4, 128), f32)
     barrier = pltpu.get_barrier_semaphore()
 
     def greet(i, carry):
@@ -337,87 +428,93 @@
         )
         return carry
 
-    lax.fori_loop(1, count, greet, 0)
-    table_copies = [
-        pltpu.make_async_copy(a, b, table_sem.at[i])
-        for i, (a, b) in enumerate(
-            ((forward_hbm, forward_ref), (plane_hbm, plane_ref), (inverse_hbm, inverse_ref))
-        )
-    ]
-    for copy in table_copies:
+    with scope("a_greet"):
+        lax.fori_loop(0, count - 1, greet, 0)
+    for copy in copies[3:]:
         copy.start()
 
     slot = lax.broadcasted_iota(jnp.int32, (1, 128), 1)
     row_of = lax.broadcasted_iota(jnp.int32, (16, 128), 0)
-    cell_x = (row_of // CY).astype(f32)
-    cell_y = (row_of % CY).astype(f32)
-    cell_z = lax.broadcasted_iota(jnp.int32, (128, 128), 0).astype(f32) - 1.0
-
-    def weights(t):
-        spot = [pos_ref[comp, pl.ds(t, 1), :] for comp in range(3)]
-        coord_x = jnp.clip(spot[0] * CX - 0.5, 0.0, CX - 1.0)
-        coord_y = jnp.clip(spot[1] * CY - 0.5, 0.0, CY - 1.0)
-        start = jnp.asarray(t, jnp.int32).astype(f32)
-        coord_z = (start + spot[2]) * span - 0.5 - start * span
-        plane = hat(coord_x, cell_x) * hat(coord_y, cell_y)
-        return plane, hat(coord_z, cell_z)
+    cell_of = row_of // 4 * share + row_of % 4
+    cell_x = jnp.where(row_of % 4 < share, cell_of // CY, -8).astype(f32)
+    cell_y = (cell_of % CY).astype(f32)
+    cell_z = lax.broadcasted_iota(jnp.int32, (near_cells, 128), 0).astype(f32) - 1.0
+    blank = jnp.zeros((128 - near_cells, 128), bf16)
 
     own = 4 * tiles
 
-    def gather(t, carry):
+    def edges(t):
+        coord_x = jnp.clip(pos_ref[0, pl.ds(t, 1), :] * CX - 0.5, 0.0, CX - 1.0)
+        coord_y = jnp.clip(pos_ref[1, pl.ds(t, 1), :] * CY - 0.5, 0.0, CY - 1.0)
+        return coord_x, coord_y
+
+    def deposit(t, carry):
         live = (slot < counts_ref[t]).astype(f32)
+        mass = mass_ref[pl.ds(t, 1), :] * live
         for comp in range(3):
             shell_ref[own + t, comp:comp + 1, :] = pos_ref[comp, pl.ds(t, 1), :]
-        shell_ref[own + t, 3:4, :] = mass_ref[pl.ds(t, 1), :] * live
+        shell_ref[own + t, 3:4, :] = mass
+        coord_x, coord_y = edges(t)
+        start = jnp.asarray(t, jnp.int32).astype(f32)
+        coord_z = (start + pos_ref[2, pl.ds(t, 1), :]) * span - 0.5 - start * span
+        plane = hat(coord_x, cell_x) * hat(coord_y, cell_y) * mass
+        high, low = halves(plane)
+        weight_high, weight_low = halves(hat(coord_z, cell_z))
+        weight_ref[t, 0] = weight_high
+        weight_ref[t, 1] = weight_low
+        rho_ref[t] = stacked_dot(
+            high,
+            low,
+            jnp.concatenate([weight_high, blank], axis=0),
+            jnp.concatenate([weight_low, blank], axis=0),
+            ((1,), (1,)),
+        )
         return carry
 
-    lax.fori_loop(0, tiles, gather, 0, unroll=4)
-    def deposit(t, carry):
-        mass = shell_ref[own + t, 3:4, :]
-        plane, wz = weights(t)
-        rho_ref[pl.ds(pl.multiple_of(t * 16, 16), 16), :] = dot3(
-            halves(plane * mass), halves(wz), ((1,), (1,))
-        )
-        return carry
-
-    lax.fori_loop(0, tiles, deposit, 0, unroll=4)
-    def swapped(x):
-        lane = lax.broadcasted_iota(jnp.int32, x.shape, 1)
-        return jnp.where(
-            (lane % width) < modes, pltpu.roll(x, 128 - modes, 1), pltpu.roll(x, modes, 1)
-        )
+    with scope("b_inwait"):
+        for copy in copies[:3]:
+            copy.wait()
+    with scope("c_deposit"):
+        lax.fori_loop(0, tiles, deposit, 0, unroll=4)
 
     quarter = lax.broadcasted_iota(jnp.int32, (8, 128), 1) // width
-
-    table_copies[0].wait()
-    rho = halves(rho_ref[...])
-
-    def transform(g, carry):
-        wide = dot3(rho, (forward_ref[0, g], forward_ref[1, g]))
-        cosine, sine = turns_ref[g], turns_ref[groups + g]
-        straight = jnp.zeros((16, 128), f32)
-        crossed = jnp.zeros((16, 128), f32)
-        for t in range(tiles):
-            part = wide[t * 16:(t + 1) * 16]
-            straight = straight + part * cosine[t:t + 1]
-            crossed = crossed + part * sine[t:t + 1]
-        lines = straight + swapped(crossed)
-        thirds = (lines[0:8], pltpu.roll(lines[0:8], 4, 0), lines[8:16])
-        for i in range(pack):
-            packed = jnp.zeros((8, 128), f32)
-            for a, third in enumerate(thirds):
-                shift = (a - i) * width % 128
-                piece = pltpu.roll(third, shift, 1) if shift else third
-                packed = jnp.where(quarter == a, piece, packed)
-            spec_ref[g * pack + i] = packed[0:4]
-        return carry
-
-    lax.fori_loop(0, groups, transform, 0)
+    lower, even_block = quarter < 2, quarter % 2 == 0
+
+    def exchange(blocks):
+        far = [pltpu.roll(b, 64, 1) for b in blocks]
+        mixed = [
+            jnp.where(lower, blocks[0], far[2]),
+            jnp.where(lower, blocks[1], far[3]),
+            jnp.where(lower, far[0], blocks[2]),
+            jnp.where(lower, far[1], blocks[3]),
+        ]
+        result = []
+        for pair in (0, 2):
+            one, two = mixed[pair], mixed[pair + 1]
+            result.append(jnp.where(even_block, one, pltpu.roll(two, width, 1)))
+            result.append(jnp.where(even_block, pltpu.roll(one, 128 - width, 1), two))
+        return result
+
+    with scope("d_tabwait"):
+        copies[3].wait()
+    with scope("e_transform"):
+        rho = [rho_ref[t] for t in range(tiles)]
+        half = tiles // 2
+        even = [rho[0]] + [rho[t] + rho[tiles - t] for t in range(1, half)] + [rho[half]]
+        odd = {t: rho[t] - rho[tiles - t] for t in range(1, half)}
+        cosines, sines = tile_waves(even, odd)
+        for g in range(groups):
+            pair = (cosines[g], sines[g]) if g else (cosines[0], cosines[half])
+            high, low = halves(jnp.concatenate(pair, axis=1))
+            lines = stacked_dot(high, low, wave_ref[0, g], wave_ref[1, g])
+            blocks = [lines[0:8], pltpu.roll(lines[0:8], 4, 0), lines[8:16], pltpu.roll(lines[8:16], 4, 0)]
+            for i, block in enumerate(exchange(blocks)):
+                spec_ref[g * pack + i] = block[0:4]
 
     def out_copy(d):
         return pltpu.make_async_remote_copy(
-            src_ref=spec_ref.at[d],
-            dst_ref=got_ref.at[me],
+            src_ref=spec_ref.at[d, pl.ds(0, share)],
+            dst_ref=got_ref.at[me, pl.ds(0, share)],
             send_sem=out_send,
             recv_sem=out_recv,
             device_id=d,
@@ -439,14 +536,15 @@
             make(other(i)).start()
             return carry
 
-        lax.fori_loop(1, count, step, 0)
-
-    def wait_all(ref, sem):
-        rest = ref.at[pl.ds(0, count - 1)]
+        lax.fori_loop(0, count - 1, step, 0)
+
+    def wait_all(rest, sem):
         pltpu.make_async_copy(rest, rest, sem).wait()
 
-    pl.semaphore_wait(barrier, count - 1)
-    start_all(out_copy)
+    with scope("f_barwait"):
+        pl.semaphore_wait(barrier, count - 1)
+    with scope("g_startout"):
+        start_all(out_copy)
     halos = []
     for step_x in (-1, 0, 1):
         for step_y in (-1, 0, 1):
@@ -463,8 +561,9 @@
                     device_id_type=MESH,
                 )
             )
-    for copy in halos:
-        copy.start()
+    with scope("h_starthalo"):
+        for copy in halos:
+            copy.start()
     got_ref[me] = spec_ref[me]
 
     ones = jnp.ones((8, 128), bf16)
@@ -477,7 +576,8 @@
             )
         return carry
 
-    lax.fori_loop(0, tiles, spread, 0)
+    with scope("i_spread"):
+        lax.fori_loop(0, tiles, spread, 0)
 
     def pairs(t, carry):
         sources = []
@@ -516,137 +616,172 @@
             short_ref[comp, pl.ds(t, 1), :] = sums[0:1, comp * 128:(comp + 1) * 128]
         return carry
 
-    depth = 3 * count * 4
-    mode_of = lax.broadcasted_iota(jnp.int32, (modes, depth), 0) + me * modes
-    packed = mode_of == 0
-    keep = jnp.where(packed, 0.0, 1.0)
-    kappa_xy, sine_x, sine_y = (lanes_ref[i:i + 1, :] for i in range(3))
-
-    def green(which):
-        kappa = kappa_xy + 4.0 * jnp.sin(which.astype(f32) * (jnp.pi / NZ)) ** 2
-        return -jnp.exp(-smoothing * kappa) / (kappa + screening)
-
-    g1 = green(mode_of)
-    g2 = green(jnp.where(packed, NZ // 2, mode_of))
-    sine_z = jnp.sin(mode_of.astype(f32) * (2.0 * jnp.pi / NZ))
-    sine_z = jnp.concatenate([sine_z, sine_z], axis=0)
-    wait_all(got_ref, out_recv)
-    table_copies[1].wait()
-    turned = jnp.transpose(got_ref[...].reshape(count * 4, 128), (1, 0))
-    mine = halves(
-        jnp.concatenate([turned[a * width:(a + 1) * width] for a in range(3)], axis=1)
-    )
-    by_cos = dot3(mine, (plane_ref[0, :depth], plane_ref[1, :depth]))
-    by_sin = dot3(mine, (plane_ref[0, depth:], plane_ref[1, depth:]))
-    cr, ci = by_cos[:modes], by_cos[modes:]
-    sr, si = by_sin[:modes], by_sin[modes:]
-    for_cos = jnp.concatenate([g1 * (keep * ci - sr), -g2 * (keep * cr + si)], axis=0)
-    for_sin = jnp.concatenate([g1 * (cr + keep * si), g2 * (ci - keep * sr)], axis=0)
-    stacked_cos = jnp.concatenate([for_cos * sine_x, for_cos * sine_y, for_cos * sine_z], axis=0)
-    stacked_sin = jnp.concatenate([for_sin * sine_x, for_sin * sine_y, for_sin * sine_z], axis=0)
-    result = dot3(halves(stacked_cos), (plane_ref[0, :depth], plane_ref[1, :depth])) + dot3(
-        halves(stacked_sin), (plane_ref[0, depth:], plane_ref[1, depth:])
-    )
-    result = jnp.concatenate([result, jnp.zeros((128 - 3 * width, depth), f32)], axis=0)
-    for a in range(3):
-        third = jnp.transpose(result[:, a * count * 4:(a + 1) * count * 4], (1, 0))
-        back_ref[:, a] = third.reshape(count, 4, 128)
-    start_all(back_copy)
+    nx, ny = rows * CX, cols * CY
+    copies[4].wait()
+    copies[5].wait()
+    with scope("i2_green"):
+        row_in = lax.broadcasted_iota(jnp.int32, (width, nx * ny), 0)
+        family, member = me // pack, me % pack
+        residue = jnp.where(
+            member < pack // 2, family, jnp.where(family == 0, tiles // 2, tiles - family)
+        )
+        mode_of = tiles * (member % (pack // 2) * modes + row_in % modes) + residue
+        alone = mode_of == 0
+        wave_z = jnp.where(alone & (row_in >= modes), NZ // 2, mode_of).astype(f32)
+        kappa = lanes_ref[0:1, :] + 4.0 * jnp.sin(wave_z * (jnp.pi / NZ)) ** 2
+        scale = jnp.where(alone, 0.5, 1.0) * (1.0 / (NZ * nx * ny))
+        green = -jnp.exp(-smoothing * kappa) / (kappa + screening) * scale
+
+    early = 0
+    with scope("j_waitgot"):
+        wait_all(got_ref.at[pl.ds(0, count - 1), pl.ds(0, share)], out_recv)
+    with scope("k_plane"):
+        copies[6].wait()
+        copies[7].wait()
+        turned = jnp.transpose(got_ref[...].reshape(count * 4, 128), (1, 0))
+        mine = jnp.concatenate(
+            [turned[a * width:(a + 1) * width] for a in range(pack)], axis=1
+        )
+        high, low = halves(mine)
+        waves = stacked_dot(high, low, into_ref[0], into_ref[1])
+        high, low = halves(waves * green)
+        high = jnp.concatenate([high] * pack, axis=0)
+        low = jnp.concatenate([low] * pack, axis=0)
+        dot = functools.partial(
+            lax.dot_general,
+            dimension_numbers=(((1,), (1,)), ((), ())),
+            preferred_element_type=f32,
+        )
+        sheet = dot(outof_ref[0], high) + dot(outof_ref[0], low) + dot(outof_ref[1], high)
+        for r in range(rows):
+            for v in range(ny // 8):
+                pick = [
+                    sheet[at:at + 8]
+                    for at in (((r * CX - 1 + b) % nx) * ny + v * 8 for b in range(pack))
+                ]
+                window = jnp.where(
+                    lower,
+                    jnp.where(even_block, pick[0], pick[1]),
+                    jnp.where(even_block, pick[2], pick[3]),
+                )
+                window_ref[r, (v + 1) * 8:(v + 2) * 8, :] = window
+                if v == 0:
+                    window_ref[r, 8 + ny:16 + ny, :] = window
+                if v == ny // 8 - 1:
+                    window_ref[r, 0:8, :] = window
+        for r in range(rows):
+            for c in range(cols):
+                d = (r // size_z * size_y + c) * size_z + r % size_z
+                back_ref[d] = window_ref[r, c * CY + 7:c * CY + 15, :]
+    with scope("l_startback"):
+        start_all(back_copy)
     home_ref[me] = back_ref[me]
 
-    for copy in halos:
-        copy.wait_recv()
-    lax.fori_loop(0, tiles, pairs, 0, unroll=2)
-    wait_all(home_ref, back_recv)
-    table_copies[2].wait()
-
-    near = quarter[0:4]
-    for g in range(groups):
-        for a in range(3):
-            blocks = [home_ref[g * pack + i, a] for i in range(pack)]
-            for f in range(3):
-                merged = jnp.zeros((4, 128), f32)
-                for i in range(pack):
-                    shift = ((i - f) * width) % 128
-                    piece = pltpu.roll(blocks[i], shift, 1) if shift else blocks[i]
-                    merged = jnp.where(near == i, piece, merged)
-                line_ref[g, f * 16 + a * 4:f * 16 + (a + 1) * 4, :] = merged
+    with scope("m_waithalo"):
+        for copy in halos:
+            copy.wait_recv()
+    with scope("n_pairs2"):
+        lax.fori_loop(early, tiles, pairs, 0, unroll=2)
+    with scope("o_waithome"):
+        wait_all(home_ref.at[pl.ds(0, count - 1)], back_recv)
+
+    with scope("p_lines"):
+        for g in range(groups):
+            lines = exchange([home_ref[g * pack + i] for i in range(pack)])
+            pulls = [lines[b - 1] - lines[b + 1] for b in (1, 2)]
+            pulls += [pltpu.roll(lines[b], 1, 0) - pltpu.roll(lines[b], 7, 0) for b in (1, 2)]
+            high, low = halves(jnp.concatenate(pulls + [lines[1], lines[2]], axis=0))
+            part = stacked_dot(high, low, wave_ref[0, g], wave_ref[1, g], ((1,), (1,)))
+            part_ref[g] = part[:, :128]
+            part_ref[groups + g] = part[:, 128:]
+    with scope("q_invert"):
         for f in range(3):
-            line_ref[g, f * 16 + 12:(f + 1) * 16, :] = jnp.zeros((4, 128), f32)
-        swap_ref[g] = swapped(line_ref[g])
-
-    together = 4
-
-    def invert(q, carry):
-        pieces = []
-        total = jnp.zeros((together * 48, 128), f32)
-        for g in range(groups):
-            line, swap = line_ref[g], swap_ref[g]
-            turned = []
-            for i in range(together):
-                t = q * together + i
-                turned.append(
-                    line * turns_ref[g, pl.ds(t, 1), :]
-                    + swap * turns_ref[groups + g, pl.ds(t, 1), :]
-                )
-            part = halves(jnp.concatenate(turned, axis=0))
-            at = slice(g * 128, (g + 1) * 128)
-            total = total + dot3(part, (inverse_ref[0, at], inverse_ref[1, at]))
-        field_ref[pl.ds(q * together, together)] = total.reshape(together, 48, 128)
-        return carry
-
-    lax.fori_loop(0, tiles // together, invert, 0)
+            at = slice(f * 16, (f + 1) * 16)
+            even = [part_ref[g, at] for g in range(groups)] + [part_ref[groups, at]]
+            odd = {g: part_ref[groups + g, at] for g in range(1, groups)}
+            cosines, sines = tile_waves(even, odd)
+            for t in range(tiles):
+                if t % half == 0:
+                    value = cosines[t]
+                elif t < half:
+                    value = cosines[t] + sines[t]
+                else:
+                    value = cosines[tiles - t] - sines[tiles - t]
+                if f == 2:
+                    value = pltpu.roll(value, 1, 1) - pltpu.roll(value, 127, 1)
+                high, low = halves(value)
+                field_ref[t, f * 16:(f + 1) * 16, :] = high
+                field_ref[t, 48 + f * 16:48 + (f + 1) * 16, :] = low
+
+    cell_near = lax.broadcasted_iota(jnp.int32, (8, 128), 0).astype(f32) - 1.0
+    copies[8].wait()
 
     def interpolate(t, carry):
-        plane, wz = weights(t)
-        here = dot3(halves(field_ref[t]), halves(wz))
+        coord_x, coord_y = edges(t)
+        left, right = hat(coord_x, 0.0), hat(coord_x, 1.0)
+        along = hat(coord_y, cell_near)
+        here = stacked_dot(
+            field_ref[t, 0:48],
+            field_ref[t, 48:96],
+            jnp.concatenate([weight_ref[t, 0], blank], axis=0),
+            jnp.concatenate([weight_ref[t, 1], blank], axis=0),
+        )
         live = (slot < counts_ref[t]).astype(f32)
         for f in range(3):
-            pull = jnp.sum(here[f * 16:(f + 1) * 16] * plane, axis=0, keepdims=True)
+            mixed = here[f * 16:f * 16 + 8] * left + here[f * 16 + 8:f * 16 + 16] * right
+            pull = jnp.sum(mixed * along, axis=0, keepdims=True)
             at = (f, pl.ds(t, 1), slice(None))
             out_ref[at] = vel_ref[at] + live * (long_kick * pull + short_kick * short_ref[at])
         return carry
 
-    lax.fori_loop(0, tiles, interpolate, 0, unroll=4)
-    for copy in halos:
-        copy.wait_send()
-    wait_all(got_ref, out_send)
-    wait_all(home_ref, back_send)
+    with scope("r_interp"):
+        lax.fori_loop(0, tiles, interpolate, 0, unroll=4)
+    with scope("s_tail"):
+        for copy in halos:
+            copy.wait_send()
+        wait_all(got_ref.at[pl.ds(0, count - 1), pl.ds(0, share)], out_send)
+        wait_all(home_ref.at[pl.ds(0, count - 1)], back_send)
 
 
 def fused_shards(sizes, positions, masses, velocities, tile_counts, neighbour_list):
     size_x, size_y, size_z, tiles, listed = sizes
     rows, cols = size_x * size_z, size_y
     count = rows * cols
-    groups = NZ // 128
+    groups = tiles // 2
+    near_cells = -(-(NZ // tiles + 3) // 16) * 16
     with jax.ensure_compile_time_eval():
-        forward, inverse, plane, turns, lanes = tables(size_x, size_y, size_z, tiles)
-    vmem = pl.BlockSpec(memory_space=pltpu.VMEM)
-    smem = pl.BlockSpec(memory_space=pltpu.SMEM)
+        wave, into, outof, lanes = tables(size_x, size_y, size_z, tiles)
     anywhere = pl.BlockSpec(memory_space=pl.ANY)
     dma = pltpu.SemaphoreType.DMA
     kicked = pl.pallas_call(
         functools.partial(kick_kernel, sizes),
         out_shape=pltpu.VMEM((3, tiles, 128), f32),
-        in_specs=[vmem] * 5 + [smem] * 2 + [anywhere] * 3,
-        out_specs=vmem,
+        in_specs=[anywhere] * 9,
+        out_specs=pl.BlockSpec(memory_space=pltpu.VMEM),
         scratch_shapes=[
-            pltpu.VMEM(forward.shape, bf16),
-            pltpu.VMEM(inverse.shape, bf16),
-            pltpu.VMEM(plane.shape, bf16),
+            pltpu.VMEM((3, tiles, 128), f32),
+            pltpu.VMEM((tiles, 128), f32),
+            pltpu.VMEM((3, tiles, 128), f32),
+            pltpu.VMEM(lanes.shape, f32),
+            pltpu.SMEM((tiles,), jnp.int32),
+            pltpu.SMEM((listed, 1, tiles), jnp.int32),
+            pltpu.VMEM(wave.shape, bf16),
+            pltpu.VMEM(into.shape, bf16),
+            pltpu.VMEM(outof.shape, bf16),
             pltpu.VMEM((9 * tiles, 4, 128), f32),
-            pltpu.VMEM((tiles * 16, 128), f32),
+            pltpu.VMEM((tiles, 16, 128), f32),
+            pltpu.VMEM((tiles, 2, near_cells, 128), bf16),
             pltpu.VMEM((count, 4, 128), f32),
             pltpu.VMEM((count, 4, 128), f32),
-            pltpu.VMEM((count, 3, 4, 128), f32),
-            pltpu.VMEM((count, 3, 4, 128), f32),
-            pltpu.VMEM((groups, 48, 128), f32),
-            pltpu.VMEM((groups, 48, 128), f32),
-            pltpu.VMEM((tiles, 48, 128), f32),
+            pltpu.VMEM((rows, cols * CY + 16, 128), f32),
+            pltpu.VMEM((count, 8, 128), f32),
+            pltpu.VMEM((count, 8, 128), f32),
+            pltpu.VMEM((2 * groups, 48, 128), f32),
+            pltpu.VMEM((tiles, 96, 128), bf16),
             pltpu.VMEM((tiles, 3, 128, 128), f32),
             pltpu.VMEM((384, 128), f32),
             pltpu.VMEM((3, tiles, 128), f32),
-            dma((3,)),
+            dma((9,)),
             dma((9,)),
             dma((9,)),
             dma,
@@ -660,13 +795,12 @@
         jnp.transpose(positions[0, 0], (1, 0, 2)),
         masses.reshape(tiles, 128),
         jnp.transpose(velocities[0, 0], (1, 0, 2)),
-        turns,
         lanes,
         tile_counts.reshape(tiles),
         jnp.transpose(neighbour_list[0], (2, 0, 1)),
-        forward,
-        inverse,
-        plane,
+        wave,
+        into,
+        outof,
     )
     return jnp.transpose(kicked, (1, 0, 2))[None, None]
 
@@ -674,10 +808,9 @@
 def fits(sizes):
     size_x, size_y, size_z, tiles, listed = sizes
     count = size_x * size_y * size_z
-    if (NZ // 2) % count or count * 4 % 128 or CX * CY > 12 or count > 64:
+    if CX != 2 or CY != 6 or count != 32 or tiles != 16 or size_y * CY % 8:
         return False
-    modes = NZ // 2 // count
-    return modes == 16 and tiles % 4 == 0
+    return NZ // 2 == 16 * count and NZ // tiles + 3 < 127
 
 
 def solution(mesh):

time: 26.7 us -> 22.3 us (0.84)
  Pallas kernels: 25.9 us -> 21.5 us
    pallas_call x1, Pallas kernels: 25.9 us -> 21.5 us  [fused_shards(): pl.pallas_call(functools.partial(kick_kernel, sizes), out_shape=pltpu.VME...]
where the time goes in v2:
time: 22.3 us; the launch traced here: 22.1 us
  Pallas kernels  21.5 us (96%)
  local copies, waits for them, and re-layouts  0.61 us (3%)
    pallas_call x1, Pallas kernels, fused_shards(): pl.pallas_call(functools.partial(kick_kernel, sizes), out_shape=pltpu.VME...  21.5 us
    unnamed x1, local copies, waits for them, and re-layouts  0.61 us

profile of v2, /device:TPU:0, one launch (start us, length us, event | category | flops | bytes accessed | tf_op | source)
XLA Modules:
  0.0 22.1 jit_solution(10592184808273737684)
XLA Ops:
  0.0 21.5 %kick.1 = f32[3,16,128]{2,1,0:T(8,128)S(1)} custom-call(f32[3,16,128]{2,1,0:T(8,128)} %bitcast.15, f32[16,128]{1,0:T(8,128)} %bitcast.17, f32[3,16,128]{2,1,0:T(8,128)} %bitcast.16, f32[8,384]{1,0:T(8,128)} %constant.8.clone.lanes_hbm, s32[16]{0:T(128)} %bitcast.19, s32[6,1,16]{2,1,0:T(1,128)} %bitcast.18, bf16[2,8,256,128]{3,2,1,0:T(8,128)(2,1)} %constant.9.clone.wave_hbm, ...), custom_call_target="tpu_custom_call" | custom-call | tf_op jit(solution)/shard_map/kick/pallas_call | solution.py:756
  21.5 0.6 %copy.11 = f32[1,1,16,3,128]{4,2,3,1,0:T(8,128)} copy(f32[1,1,16,3,128]{4,2,3,1,0:T(8,128)S(1)} %bitcast.14) | data formatting | bytes 49152

commit v3 on v2

--- a/solution.py
+++ b/solution.py
@@ -313,7 +313,11 @@
     outof = cas(wave_x, wave_y)
     lanes = np.zeros((8, nx * ny))
     lanes[:] = 4 * np.sin(np.pi * wave_x / nx) ** 2 + 4 * np.sin(np.pi * wave_y / ny) ** 2
-    return np_halves(np.stack(waves)), np_halves(into), np_halves(outof), jnp.asarray(lanes, f32)
+    return np_halves(np.stack(waves)), np_halves(lane_tiles(into)), np_halves(lane_tiles(outof)), jnp.asarray(lanes, f32)
+
+
+def lane_tiles(table):
+    return np.stack(np.split(table, table.shape[1] // 128, axis=1))
 
 
 def tile_waves(even, odd):
@@ -364,7 +368,7 @@
     out_ref,
     pos_ref, mass_ref, vel_ref, lanes_ref, counts_ref, list_ref, wave_ref, into_ref, outof_ref,
     shell_ref, rho_ref, weight_ref, spec_ref, got_ref, window_ref,
-    back_ref, home_ref, part_ref, field_ref, spread_ref, accum_ref, short_ref,
+    back_ref, home_ref, part_ref, field_ref, spread_ref, theirs_0, theirs_1, pull_0, pull_1, strength_0, strength_1, short_ref,
     input_sem, halo_send, halo_recv, out_send, out_recv, back_send, back_recv,
 ):
     size_x, size_y, size_z, tiles, listed = sizes
@@ -409,27 +413,33 @@
     third = size_x - 1 - second
     spot_here = gy * size_z + gz
 
-    def other(i):
-        if size_x != 4:
-            return lax.rem(me + 1 + i, count)
-        block = i // flat
-        away = lax.rem(i, flat) + jnp.where(block == 3, 1, 0)
-        plane = jnp.where(
-            block == 0, first, jnp.where(block == 1, second, jnp.where(block == 2, third, gx))
-        )
-        return plane * flat + lax.rem(spot_here + away, flat)
+    turns = [lax.rem(spot_here + i, flat) for i in range(flat)]
+
+    def for_others(act):
+        def some(members):
+            def step(p, carry):
+                if size_x == 4:
+                    plane = jnp.where(
+                        p == 0, first, jnp.where(p == 1, second, jnp.where(p == 2, third, gx))
+                    )
+                else:
+                    plane = lax.rem(gx + p + 1, size_x)
+                for i in members:
+                    act(plane * flat + turns[i])
+                return carry
+
+            return step
+
+        lax.fori_loop(0, size_x, some(range(1, flat)), 0)
+        lax.fori_loop(0, size_x - 1, some(range(1)), 0)
 
     got_ref[...] = jnp.zeros((count, 4, 128), f32)
     barrier = pltpu.get_barrier_semaphore()
 
-    def greet(i, carry):
-        pl.semaphore_signal(
-            barrier, inc=1, device_id=other(i), device_id_type=LOGICAL
-        )
-        return carry
-
     with scope("a_greet"):
-        lax.fori_loop(0, count - 1, greet, 0)
+        for_others(
+            lambda d: pl.semaphore_signal(barrier, inc=1, device_id=d, device_id_type=LOGICAL)
+        )
     for copy in copies[3:]:
         copy.start()
 
@@ -532,11 +542,7 @@
         )
 
     def start_all(make):
-        def step(i, carry):
-            make(other(i)).start()
-            return carry
-
-        lax.fori_loop(0, count - 1, step, 0)
+        for_others(lambda d: make(d).start())
 
     def wait_all(rest, sem):
         pltpu.make_async_copy(rest, rest, sem).wait()
@@ -566,55 +572,82 @@
             copy.start()
     got_ref[me] = spec_ref[me]
 
-    ones = jnp.ones((8, 128), bf16)
-    block = 32
+    theirs, pulls, strengths = (theirs_0, theirs_1), (pull_0, pull_1), (strength_0, strength_1)
+    line_of = lax.broadcasted_iota(jnp.int32, (8, 128), 0)
+    first_lines, one_line = line_of < 3, line_of == 3
+    square_lines = (line_of > 3) & (line_of < 7)
+
+    def thirds(x):
+        high = x.astype(bf16).astype(f32)
+        rest = x - high
+        middle = rest.astype(bf16).astype(f32)
+        return high, middle, rest - middle
 
     def spread(t, carry):
-        for comp in range(3):
-            spread_ref[t, comp] = jnp.transpose(
-                jnp.broadcast_to(pos_ref[comp, pl.ds(t, 1), :], (128, 128)), (1, 0)
-            )
+        tile = shell_ref[own + t]
+        spot = jnp.where(first_lines, jnp.concatenate([tile, tile], axis=0) - 0.5, 0.0)
+        norm = jnp.sum(spot * spot, axis=0, keepdims=True) + softening
+        mine = jnp.where(one_line, norm, jnp.where(square_lines, 1.0, -2.0 * spot))
+        high, middle, low = thirds(mine)
+        terms = [high, high, middle, high, low, middle, jnp.zeros((80, 128), f32)]
+        spread_ref[t] = jnp.transpose(jnp.concatenate(terms, axis=0), (1, 0)).astype(bf16)
         return carry
 
     with scope("i_spread"):
-        lax.fori_loop(0, tiles, spread, 0)
-
-    def pairs(t, carry):
-        sources = []
+        lax.fori_loop(0, tiles, spread, 0, unroll=2)
+
+    def describe(t, theirs_ref, pull_ref):
         for n in range(listed):
             entry = list_ref[n, 0, t]
-            group, layer = entry // tiles, entry % tiles
-            away = (layer - t + 1 + tiles) % tiles - 1
+            group = lax.div(entry, tiles)
+            layer = entry - group * tiles
+            step_x = lax.div(group * 11, 32)
+            step_y = group - 3 * step_x
+            away = lax.rem(layer - t + 1 + tiles, tiles)
             tile = shell_ref[entry]
-            sources.append(
-                (
-                    tile[0:1] + (group // 3 - 1).astype(f32),
-                    tile[1:2] + (group % 3 - 1).astype(f32),
-                    tile[2:3] + away.astype(f32),
-                    tile[3:4],
-                )
+            shift = jnp.where(
+                line_of % 4 == 0,
+                step_x.astype(f32),
+                jnp.where(line_of % 4 == 1, step_y.astype(f32), away.astype(f32)),
             )
-        for b in range(128 // block):
-            here = [spread_ref[t, comp, b * block:(b + 1) * block, :] for comp in range(3)]
-            totals = [jnp.zeros((block, 128), f32) for comp in range(3)]
-            for source in sources:
-                parts = [source[comp] - here[comp] for comp in range(3)]
-                square = parts[0] * parts[0] + parts[1] * parts[1] + parts[2] * parts[2]
-                root = lax.rsqrt(square + softening)
-                strength = source[3] * jnp.exp2(square * (-1.0 / (split_scale * math.log(2.0)))) * (root * root * root)
-                totals = [totals[comp] + strength * parts[comp] for comp in range(3)]
-            for comp in range(3):
-                accum_ref[comp * 128 + b * block:comp * 128 + (b + 1) * block, :] = totals[comp]
-        high, low = halves(accum_ref[...])
-        dot = functools.partial(
-            lax.dot_general,
-            dimension_numbers=(((1,), (1,)), ((), ())),
-            preferred_element_type=f32,
-        )
-        sums = dot(ones, high) + dot(ones, low)
-        for comp in range(3):
-            short_ref[comp, pl.ds(t, 1), :] = sums[0:1, comp * 128:(comp + 1) * 128]
-        return carry
+            spot = jnp.concatenate([tile, tile], axis=0) + (shift - 1.5)
+            theirs = jnp.where(
+                first_lines, spot, jnp.where(one_line, 1.0, jnp.where(square_lines, spot * spot, 0.0))
+            )
+            high, middle, low = thirds(theirs)
+            one = jnp.concatenate([high, middle], axis=0).astype(bf16)
+            two = jnp.concatenate([high, low], axis=0).astype(bf16)
+            theirs_ref[n] = jnp.concatenate([one, two, one], axis=0)
+            pull = jnp.concatenate(halves(theirs * tile[3:4]), axis=0)
+            pull_ref[n] = pull
+
+    product = functools.partial(lax.dot_general, preferred_element_type=f32)
+
+    def attract(t, theirs_ref, strength_ref):
+        for n in range(0, listed, 2):
+            square = product(
+                spread_ref[t][:, :48],
+                jnp.concatenate([theirs_ref[n], theirs_ref[n + 1]], axis=1),
+                (((1,), (0,)), ((), ())),
+            )
+            root = lax.rsqrt(square)
+            strength = jnp.exp2(square * (-1.0 / (split_scale * math.log(2.0)))) * (root * root * root)
+            high, low = halves(strength)
+            for k in range(2):
+                at = slice(k * 128, (k + 1) * 128)
+                strength_ref[2 * (n + k)] = high[:, at]
+                strength_ref[2 * (n + k) + 1] = low[:, at]
+
+    def collect(t, pull_ref, strength_ref):
+        total = product(
+            jnp.concatenate([strength_ref[i] for i in range(2 * listed)], axis=1),
+            jnp.concatenate([pull_ref[i // 2] for i in range(2 * listed)], axis=1),
+             (((1,), (1,)), ((), ())))
+        total = jnp.transpose(total, (1, 0))
+        total = total[0:8] + total[8:16]
+        tile = shell_ref[own + t]
+        spot = jnp.concatenate([tile, tile], axis=0) - 0.5
+        short_ref[t] = (total - spot * total[3:4]) * (short_kick * math.exp(softening / split_scale))
 
     nx, ny = rows * CX, cols * CY
     copies[4].wait()
@@ -632,7 +665,6 @@
         scale = jnp.where(alone, 0.5, 1.0) * (1.0 / (NZ * nx * ny))
         green = -jnp.exp(-smoothing * kappa) / (kappa + screening) * scale
 
-    early = 0
     with scope("j_waitgot"):
         wait_all(got_ref.at[pl.ds(0, count - 1), pl.ds(0, share)], out_recv)
     with scope("k_plane"):
@@ -643,7 +675,8 @@
             [turned[a * width:(a + 1) * width] for a in range(pack)], axis=1
         )
         high, low = halves(mine)
-        waves = stacked_dot(high, low, into_ref[0], into_ref[1])
+        joined = lambda ref, part: jnp.concatenate([ref[part, i] for i in range(nx * ny // 128)], axis=1)
+        waves = stacked_dot(high, low, joined(into_ref, 0), joined(into_ref, 1))
         high, low = halves(waves * green)
         high = jnp.concatenate([high] * pack, axis=0)
         low = jnp.concatenate([low] * pack, axis=0)
@@ -652,7 +685,7 @@
             dimension_numbers=(((1,), (1,)), ((), ())),
             preferred_element_type=f32,
         )
-        sheet = dot(outof_ref[0], high) + dot(outof_ref[0], low) + dot(outof_ref[1], high)
+        sheet = dot(joined(outof_ref, 0), high) + dot(joined(outof_ref, 0), low) + dot(joined(outof_ref, 1), high)
         for r in range(rows):
             for v in range(ny // 8):
                 pick = [
@@ -680,8 +713,18 @@
     with scope("m_waithalo"):
         for copy in halos:
             copy.wait_recv()
-    with scope("n_pairs2"):
-        lax.fori_loop(early, tiles, pairs, 0, unroll=2)
+    def pairs(k, carry):
+        for odd in (0, 1):
+            t = 2 * k + odd
+            attract(t, theirs[odd], strengths[odd])
+            collect(lax.rem(t + tiles - 1, tiles), pulls[1 - odd], strengths[1 - odd])
+            describe(lax.rem(t + 1, tiles), theirs[1 - odd], pulls[1 - odd])
+        return carry
+
+    with scope("n_pairs"):
+        describe(0, theirs[0], pulls[0])
+        lax.fori_loop(0, tiles // 2, pairs, 0)
+        collect(tiles - 1, pulls[1], strengths[1])
     with scope("o_waithome"):
         wait_all(home_ref.at[pl.ds(0, count - 1)], back_recv)
 
@@ -731,7 +774,7 @@
             mixed = here[f * 16:f * 16 + 8] * left + here[f * 16 + 8:f * 16 + 16] * right
             pull = jnp.sum(mixed * along, axis=0, keepdims=True)
             at = (f, pl.ds(t, 1), slice(None))
-            out_ref[at] = vel_ref[at] + live * (long_kick * pull + short_kick * short_ref[at])
+            out_ref[at] = vel_ref[at] + live * (long_kick * pull + short_ref[t, f:f + 1, :])
         return carry
 
     with scope("r_interp"):
@@ -778,9 +821,14 @@
             pltpu.VMEM((count, 8, 128), f32),
             pltpu.VMEM((2 * groups, 48, 128), f32),
             pltpu.VMEM((tiles, 96, 128), bf16),
-            pltpu.VMEM((tiles, 3, 128, 128), f32),
-            pltpu.VMEM((384, 128), f32),
-            pltpu.VMEM((3, tiles, 128), f32),
+            pltpu.VMEM((tiles, 128, 128), bf16),
+            pltpu.VMEM((listed, 48, 128), bf16),
+            pltpu.VMEM((listed, 48, 128), bf16),
+            pltpu.VMEM((listed, 16, 128), bf16),
+            pltpu.VMEM((listed, 16, 128), bf16),
+            pltpu.VMEM((2 * listed, 128, 128), bf16),
+            pltpu.VMEM((2 * listed, 128, 128), bf16),
+            pltpu.VMEM((tiles, 8, 128), f32),
             dma((9,)),
             dma((9,)),
             dma((9,)),

time: 22.3 us -> 21 us (0.942)
  Pallas kernels: 21.5 us -> 20.2 us
    pallas_call x1, Pallas kernels: 21.5 us -> 20.2 us  [fused_shards(): pl.pallas_call(functools.partial(kick_kernel, sizes), out_shape=pltpu.VME...]
where the time goes in v3:
time: 21 us; the launch traced here: 20.9 us
  Pallas kernels  20.2 us (96%)
  local copies, waits for them, and re-layouts  0.61 us (3%)
    pallas_call x1, Pallas kernels, fused_shards(): pl.pallas_call(functools.partial(kick_kernel, sizes), out_shape=pltpu.VME...  20.2 us
    unnamed x1, local copies, waits for them, and re-layouts  0.61 us

profile of v3, /device:TPU:0, one launch (start us, length us, event | category | flops | bytes accessed | tf_op | source)
XLA Modules:
  0.0 20.9 jit_solution(14503539820419537040)
XLA Ops:
  0.0 20.2 %kick.1 = f32[3,16,128]{2,1,0:T(8,128)S(1)} custom-call(f32[3,16,128]{2,1,0:T(8,128)} %bitcast.15, f32[16,128]{1,0:T(8,128)} %bitcast.17, f32[3,16,128]{2,1,0:T(8,128)} %bitcast.16, f32[8,384]{1,0:T(8,128)} %constant.8.clone.lanes_hbm, s32[16]{0:T(128)} %bitcast.19, s32[6,1,16]{2,1,0:T(1,128)} %bitcast.18, bf16[2,8,256,128]{3,2,1,0:T(8,128)(2,1)} %constant.9.clone.wave_hbm, ...), custom_call_target="tpu_custom_call" | custom-call | tf_op jit(solution)/shard_map/kick/pallas_call | solution.py:799
  20.2 0.6 %copy.11 = f32[1,1,16,3,128]{4,2,3,1,0:T(8,128)} copy(f32[1,1,16,3,128]{4,2,3,1,0:T(8,128)S(1)} %bitcast.14) | data formatting | bytes 49152

commit v4 on v3

--- a/solution.py
+++ b/solution.py
@@ -263,6 +263,24 @@
     rows = high.shape[0]
     both = dot(jnp.concatenate([high, low], axis=0), table_high)
     return both[:rows] + both[rows:] + dot(high, table_low)
+
+
+def joint_dot(high, low, table_high, table_low):
+    rows = high.shape[0]
+    left = jnp.concatenate(
+        [
+            jnp.concatenate([high, high], axis=1),
+            jnp.concatenate([low, jnp.zeros_like(low)], axis=1),
+        ],
+        axis=0,
+    )
+    both = lax.dot_general(
+        left,
+        jnp.concatenate([table_high, table_low], axis=0),
+        (((1,), (0,)), ((), ())),
+        preferred_element_type=f32,
+    )
+    return both[:rows] + both[rows:]
 
 
 def tables(size_x, size_y, size_z, tiles):
@@ -313,7 +331,9 @@
     outof = cas(wave_x, wave_y)
     lanes = np.zeros((8, nx * ny))
     lanes[:] = 4 * np.sin(np.pi * wave_x / nx) ** 2 + 4 * np.sin(np.pi * wave_y / ny) ** 2
-    return np_halves(np.stack(waves)), np_halves(lane_tiles(into)), np_halves(lane_tiles(outof)), jnp.asarray(lanes, f32)
+    waves = np.stack(waves)
+    unwaves = waves.reshape(groups, 2, 128, 128).transpose(0, 1, 3, 2)
+    return np_halves(waves), np_halves(unwaves), np_halves(lane_tiles(into)), np_halves(lane_tiles(outof)), jnp.asarray(lanes, f32)
 
 
 def lane_tiles(table):
@@ -364,9 +384,9 @@
 
 def kick_kernel(
     sizes,
-    pos_hbm, mass_hbm, vel_hbm, lanes_hbm, counts_hbm, list_hbm, wave_hbm, into_hbm, outof_hbm,
+    pos_hbm, mass_hbm, vel_hbm, lanes_hbm, counts_hbm, list_hbm, wave_hbm, into_hbm, outof_hbm, unwave_hbm,
     out_ref,
-    pos_ref, mass_ref, vel_ref, lanes_ref, counts_ref, list_ref, wave_ref, into_ref, outof_ref,
+    pos_ref, mass_ref, vel_ref, lanes_ref, counts_ref, list_ref, wave_ref, into_ref, outof_ref, unwave_ref,
     shell_ref, rho_ref, weight_ref, spec_ref, got_ref, window_ref,
     back_ref, home_ref, part_ref, field_ref, spread_ref, theirs_0, theirs_1, pull_0, pull_1, strength_0, strength_1, short_ref,
     input_sem, halo_send, halo_recv, out_send, out_recv, back_send, back_recv,
@@ -399,6 +419,7 @@
                 (into_hbm, into_ref),
                 (outof_hbm, outof_ref),
                 (vel_hbm, vel_ref),
+                (unwave_hbm, unwave_ref),
             )
         )
     ]
@@ -685,7 +706,10 @@
             dimension_numbers=(((1,), (1,)), ((), ())),
             preferred_element_type=f32,
         )
-        sheet = dot(joined(outof_ref, 0), high) + dot(joined(outof_ref, 0), low) + dot(joined(outof_ref, 1), high)
+        sheet = dot(
+            jnp.concatenate([joined(outof_ref, 0), joined(outof_ref, 0), joined(outof_ref, 1)], axis=1),
+            jnp.concatenate([high, low, high], axis=1),
+        )
         for r in range(rows):
             for v in range(ny // 8):
                 pick = [
@@ -723,18 +747,24 @@
 
     with scope("n_pairs"):
         describe(0, theirs[0], pulls[0])
-        lax.fori_loop(0, tiles // 2, pairs, 0)
+        lax.fori_loop(0, tiles // 2, pairs, 0, unroll=4)
         collect(tiles - 1, pulls[1], strengths[1])
     with scope("o_waithome"):
         wait_all(home_ref.at[pl.ds(0, count - 1)], back_recv)
 
+    copies[9].wait()
     with scope("p_lines"):
         for g in range(groups):
             lines = exchange([home_ref[g * pack + i] for i in range(pack)])
             pulls = [lines[b - 1] - lines[b + 1] for b in (1, 2)]
             pulls += [pltpu.roll(lines[b], 1, 0) - pltpu.roll(lines[b], 7, 0) for b in (1, 2)]
             high, low = halves(jnp.concatenate(pulls + [lines[1], lines[2]], axis=0))
-            part = stacked_dot(high, low, wave_ref[0, g], wave_ref[1, g], ((1,), (1,)))
+            part = joint_dot(
+                high,
+                low,
+                jnp.concatenate([unwave_ref[0, g, 0], unwave_ref[0, g, 1]], axis=1),
+                jnp.concatenate([unwave_ref[1, g, 0], unwave_ref[1, g, 1]], axis=1),
+            )
             part_ref[g] = part[:, :128]
             part_ref[groups + g] = part[:, 128:]
     with scope("q_invert"):
@@ -778,7 +808,7 @@
         return carry
 
     with scope("r_interp"):
-        lax.fori_loop(0, tiles, interpolate, 0, unroll=4)
+        lax.fori_loop(0, tiles, interpolate, 0, unroll=16)
     with scope("s_tail"):
         for copy in halos:
             copy.wait_send()
@@ -793,13 +823,13 @@
     groups = tiles // 2
     near_cells = -(-(NZ // tiles + 3) // 16) * 16
     with jax.ensure_compile_time_eval():
-        wave, into, outof, lanes = tables(size_x, size_y, size_z, tiles)
+        wave, unwave, into, outof, lanes = tables(size_x, size_y, size_z, tiles)
     anywhere = pl.BlockSpec(memory_space=pl.ANY)
     dma = pltpu.SemaphoreType.DMA
     kicked = pl.pallas_call(
         functools.partial(kick_kernel, sizes),
         out_shape=pltpu.VMEM((3, tiles, 128), f32),
-        in_specs=[anywhere] * 9,
+        in_specs=[anywhere] * 10,
         out_specs=pl.BlockSpec(memory_space=pltpu.VMEM),
         scratch_shapes=[
             pltpu.VMEM((3, tiles, 128), f32),
@@ -811,6 +841,7 @@
             pltpu.VMEM(wave.shape, bf16),
             pltpu.VMEM(into.shape, bf16),
             pltpu.VMEM(outof.shape, bf16),
+            pltpu.VMEM(unwave.shape, bf16),
             pltpu.VMEM((9 * tiles, 4, 128), f32),
             pltpu.VMEM((tiles, 16, 128), f32),
             pltpu.VMEM((tiles, 2, near_cells, 128), bf16),
@@ -829,7 +860,7 @@
             pltpu.VMEM((2 * listed, 128, 128), bf16),
             pltpu.VMEM((2 * listed, 128, 128), bf16),
             pltpu.VMEM((tiles, 8, 128), f32),
-            dma((9,)),
+            dma((10,)),
             dma((9,)),
             dma((9,)),
             dma,
@@ -849,6 +880,7 @@
         wave,
         into,
         outof,
+        unwave,
     )
     return jnp.transpose(kicked, (1, 0, 2))[None, None]
 

time: 21 us -> 20.1 us (0.957)
  Pallas kernels: 20.2 us -> 19.3 us
    pallas_call x1, Pallas kernels: 20.2 us -> 19.3 us  [fused_shards(): pl.pallas_call(functools.partial(kick_kernel, sizes), out_shape=pltpu.VME...]
where the time goes in v4:
time: 20.1 us; the launch traced here: 19.9 us
  Pallas kernels  19.3 us (96%)
  local copies, waits for them, and re-layouts  0.61 us (3%)
    pallas_call x1, Pallas kernels, fused_shards(): pl.pallas_call(functools.partial(kick_kernel, sizes), out_shape=pltpu.VME...  19.3 us
    unnamed x1, local copies, waits for them, and re-layouts  0.61 us

profile of v4, /device:TPU:0, one launch (start us, length us, event | category | flops | bytes accessed | tf_op | source)
XLA Modules:
  0.0 19.9 jit_solution(7417727951777866345)
XLA Ops:
  0.0 19.3 %kick.1 = f32[3,16,128]{2,1,0:T(8,128)S(1)} custom-call(f32[3,16,128]{2,1,0:T(8,128)} %bitcast.15, f32[16,128]{1,0:T(8,128)} %bitcast.17, f32[3,16,128]{2,1,0:T(8,128)} %bitcast.16, f32[8,384]{1,0:T(8,128)} %constant.10.clone.lanes_hbm, s32[16]{0:T(128)} %bitcast.19, s32[6,1,16]{2,1,0:T(1,128)} %bitcast.18, ...), custom_call_target="tpu_custom_call" | custom-call | tf_op jit(solution)/shard_map/kick/pallas_call | solution.py:829
  19.3 0.6 %copy.12 = f32[1,1,16,3,128]{4,2,3,1,0:T(8,128)} copy(f32[1,1,16,3,128]{4,2,3,1,0:T(8,128)S(1)} %bitcast.14) | data formatting | bytes 49152

commit v5 on v4

--- a/solution.py
+++ b/solution.py
@@ -557,7 +557,7 @@
             src_ref=back_ref.at[d],
             dst_ref=home_ref.at[me],
             send_sem=back_send,
-            recv_sem=back_recv,
+            recv_sem=back_recv.at[me // (count // 2)],
             device_id=d,
             device_id_type=LOGICAL,
         )
@@ -699,17 +699,8 @@
         joined = lambda ref, part: jnp.concatenate([ref[part, i] for i in range(nx * ny // 128)], axis=1)
         waves = stacked_dot(high, low, joined(into_ref, 0), joined(into_ref, 1))
         high, low = halves(waves * green)
-        high = jnp.concatenate([high] * pack, axis=0)
-        low = jnp.concatenate([low] * pack, axis=0)
-        dot = functools.partial(
-            lax.dot_general,
-            dimension_numbers=(((1,), (1,)), ((), ())),
-            preferred_element_type=f32,
-        )
-        sheet = dot(
-            jnp.concatenate([joined(outof_ref, 0), joined(outof_ref, 0), joined(outof_ref, 1)], axis=1),
-            jnp.concatenate([high, low, high], axis=1),
-        )
+        plane = stacked_dot(high, low, joined(outof_ref, 0), joined(outof_ref, 1))
+        sheet = jnp.transpose(jnp.concatenate([plane] * pack, axis=0), (1, 0))
         for r in range(rows):
             for v in range(ny // 8):
                 pick = [
@@ -732,7 +723,10 @@
                 back_ref[d] = window_ref[r, c * CY + 7:c * CY + 15, :]
     with scope("l_startback"):
         start_all(back_copy)
-    home_ref[me] = back_ref[me]
+    kept = pltpu.make_async_copy(
+        back_ref.at[me], home_ref.at[me], back_recv.at[me // (count // 2)]
+    )
+    kept.start()
 
     with scope("m_waithalo"):
         for copy in halos:
@@ -749,13 +743,15 @@
         describe(0, theirs[0], pulls[0])
         lax.fori_loop(0, tiles // 2, pairs, 0, unroll=4)
         collect(tiles - 1, pulls[1], strengths[1])
-    with scope("o_waithome"):
-        wait_all(home_ref.at[pl.ds(0, count - 1)], back_recv)
-
     copies[9].wait()
-    with scope("p_lines"):
-        for g in range(groups):
-            lines = exchange([home_ref[g * pack + i] for i in range(pack)])
+
+    def untwist(h, carry):
+        near = (me // (count // 2) + h) % 2
+        with scope("o_waithome"):
+            wait_all(home_ref.at[pl.ds(0, count // 2)], back_recv.at[near])
+        for i in range(groups // 2):
+            g = near * (groups // 2) + i
+            lines = exchange([home_ref[g * pack + k] for k in range(pack)])
             pulls = [lines[b - 1] - lines[b + 1] for b in (1, 2)]
             pulls += [pltpu.roll(lines[b], 1, 0) - pltpu.roll(lines[b], 7, 0) for b in (1, 2)]
             high, low = halves(jnp.concatenate(pulls + [lines[1], lines[2]], axis=0))
@@ -767,6 +763,10 @@
             )
             part_ref[g] = part[:, :128]
             part_ref[groups + g] = part[:, 128:]
+        return carry
+
+    with scope("p_lines"):
+        lax.fori_loop(0, 2, untwist, 0)
     with scope("q_invert"):
         for f in range(3):
             at = slice(f * 16, (f + 1) * 16)
@@ -866,7 +866,7 @@
             dma,
             dma,
             dma,
-            dma,
+            dma((2,)),
         ],
         compiler_params=pltpu.CompilerParams(collective_id=0, has_side_effects=True),
         name="kick",

time: 20.1 us -> 19.7 us (0.980)
  Pallas kernels: 19.3 us -> 19 us
    pallas_call x1, Pallas kernels: 19.3 us -> 19 us  [fused_shards(): pl.pallas_call(functools.partial(kick_kernel, sizes), out_shape=pltpu.VME...]
where the time goes in v5:
time: 19.7 us; the launch traced here: 19.6 us
  Pallas kernels  19 us (96%)
  local copies, waits for them, and re-layouts  0.61 us (3%)
    pallas_call x1, Pallas kernels, fused_shards(): pl.pallas_call(functools.partial(kick_kernel, sizes), out_shape=pltpu.VME...  19 us
    unnamed x1, local copies, waits for them, and re-layouts  0.61 us

profile of v5, /device:TPU:0, one launch (start us, length us, event | category | flops | bytes accessed | tf_op | source)
XLA Modules:
  0.0 19.6 jit_solution(18400929556926845600)
XLA Ops:
  0.0 19.0 %kick.1 = f32[3,16,128]{2,1,0:T(8,128)S(1)} custom-call(f32[3,16,128]{2,1,0:T(8,128)} %bitcast.15, f32[16,128]{1,0:T(8,128)} %bitcast.17, f32[3,16,128]{2,1,0:T(8,128)} %bitcast.16, f32[8,384]{1,0:T(8,128)} %constant.10.clone.lanes_hbm, s32[16]{0:T(128)} %bitcast.19, s32[6,1,16]{2,1,0:T(1,128)} %bitcast.18, ...), custom_call_target="tpu_custom_call" | custom-call | tf_op jit(solution)/shard_map/kick/pallas_call | solution.py:829
  19.0 0.6 %copy.12 = f32[1,1,16,3,128]{4,2,3,1,0:T(8,128)} copy(f32[1,1,16,3,128]{4,2,3,1,0:T(8,128)S(1)} %bitcast.14) | data formatting | bytes 49152

commit v6 on v5

--- a/solution.py
+++ b/solution.py
@@ -333,6 +333,8 @@
     lanes[:] = 4 * np.sin(np.pi * wave_x / nx) ** 2 + 4 * np.sin(np.pi * wave_y / ny) ** 2
     waves = np.stack(waves)
     unwaves = waves.reshape(groups, 2, 128, 128).transpose(0, 1, 3, 2)
+    near_cells = -(-(NZ // tiles + 3) // 16) * 16
+    waves = waves.reshape(groups, 2, 128, 128)[:, :, :near_cells]
     return np_halves(waves), np_halves(unwaves), np_halves(lane_tiles(into)), np_halves(lane_tiles(outof)), jnp.asarray(lanes, f32)
 
 
@@ -537,7 +539,11 @@
         for g in range(groups):
             pair = (cosines[g], sines[g]) if g else (cosines[0], cosines[half])
             high, low = halves(jnp.concatenate(pair, axis=1))
-            lines = stacked_dot(high, low, wave_ref[0, g], wave_ref[1, g])
+            waves = [
+                jnp.concatenate([wave_ref[part, g, 0], blank, wave_ref[part, g, 1], blank], axis=0)
+                for part in range(2)
+            ]
+            lines = stacked_dot(high, low, waves[0], waves[1])
             blocks = [lines[0:8], pltpu.roll(lines[0:8], 4, 0), lines[8:16], pltpu.roll(lines[8:16], 4, 0)]
             for i, block in enumerate(exchange(blocks)):
                 spec_ref[g * pack + i] = block[0:4]
@@ -588,9 +594,6 @@
                     device_id_type=MESH,
                 )
             )
-    with scope("h_starthalo"):
-        for copy in halos:
-            copy.start()
     got_ref[me] = spec_ref[me]
 
     theirs, pulls, strengths = (theirs_0, theirs_1), (pull_0, pull_1), (strength_0, strength_1)
@@ -615,7 +618,12 @@
         return carry
 
     with scope("i_spread"):
-        lax.fori_loop(0, tiles, spread, 0, unroll=2)
+        lax.fori_loop(0, tiles // 2, spread, 0, unroll=2)
+    with scope("h_starthalo"):
+        for copy in halos:
+            copy.start()
+    with scope("i_spreadb"):
+        lax.fori_loop(tiles // 2, tiles, spread, 0, unroll=2)
 
     def describe(t, theirs_ref, pull_ref):
         for n in range(listed):
@@ -741,7 +749,7 @@
 
     with scope("n_pairs"):
         describe(0, theirs[0], pulls[0])
-        lax.fori_loop(0, tiles // 2, pairs, 0, unroll=4)
+        lax.fori_loop(0, tiles // 2, pairs, 0, unroll=8)
         collect(tiles - 1, pulls[1], strengths[1])
     copies[9].wait()
 

time: 19.7 us -> 19.6 us (level)
  no operation moved by 1% of the time
where the time goes in v6:
time: 19.6 us; the launch traced here: 19.5 us
  Pallas kernels  18.9 us (96%)
  local copies, waits for them, and re-layouts  0.61 us (3%)
    pallas_call x1, Pallas kernels, fused_shards(): pl.pallas_call(functools.partial(kick_kernel, sizes), out_shape=pltpu.VME...  18.9 us
    unnamed x1, local copies, waits for them, and re-layouts  0.61 us

profile of v6, /device:TPU:0, one launch (start us, length us, event | category | flops | bytes accessed | tf_op | source)
XLA Modules:
  0.0 19.5 jit_solution(17675942490174211853)
XLA Ops:
  0.0 18.9 %kick.1 = f32[3,16,128]{2,1,0:T(8,128)S(1)} custom-call(f32[3,16,128]{2,1,0:T(8,128)} %bitcast.15, f32[16,128]{1,0:T(8,128)} %bitcast.17, f32[3,16,128]{2,1,0:T(8,128)} %bitcast.16, f32[8,384]{1,0:T(8,128)} %constant.10.clone.lanes_hbm, s32[16]{0:T(128)} %bitcast.19, s32[6,1,16]{2,1,0:T(1,128)} %bitcast.18, ...), custom_call_target="tpu_custom_call" | custom-call | tf_op jit(solution)/shard_map/kick/pallas_call | solution.py:837
  18.9 0.6 %copy.12 = f32[1,1,16,3,128]{4,2,3,1,0:T(8,128)} copy(f32[1,1,16,3,128]{4,2,3,1,0:T(8,128)S(1)} %bitcast.14) | data formatting | bytes 49152

commit v7 on v6

--- a/solution.py
+++ b/solution.py
@@ -425,9 +425,6 @@
             )
         )
     ]
-    for copy in copies[:3]:
-        copy.start()
-
     def place(r, c):
         return (r // size_z, c, r % size_z)
 
@@ -463,7 +460,7 @@
         for_others(
             lambda d: pl.semaphore_signal(barrier, inc=1, device_id=d, device_id_type=LOGICAL)
         )
-    for copy in copies[3:]:
+    for copy in copies:
         copy.start()
 
     slot = lax.broadcasted_iota(jnp.int32, (1, 128), 1)

time: 19.6 us -> 19.6 us (level)
  no operation moved by 1% of the time
where the time goes in v7:
time: 19.6 us; the launch traced here: 19.5 us
  Pallas kernels  18.9 us (96%)
  local copies, waits for them, and re-layouts  0.61 us (3%)
    pallas_call x1, Pallas kernels, fused_shards(): pl.pallas_call(functools.partial(kick_kernel, sizes), out_shape=pltpu.VME...  18.9 us
    unnamed x1, local copies, waits for them, and re-layouts  0.61 us

profile of v7, /device:TPU:0, one launch (start us, length us, event | category | flops | bytes accessed | tf_op | source)
XLA Modules:
  0.0 19.5 jit_solution(4302240273290130508)
XLA Ops:
  0.0 18.9 %kick.1 = f32[3,16,128]{2,1,0:T(8,128)S(1)} custom-call(f32[3,16,128]{2,1,0:T(8,128)} %bitcast.15, f32[16,128]{1,0:T(8,128)} %bitcast.17, f32[3,16,128]{2,1,0:T(8,128)} %bitcast.16, f32[8,384]{1,0:T(8,128)} %constant.10.clone.lanes_hbm, s32[16]{0:T(128)} %bitcast.19, s32[6,1,16]{2,1,0:T(1,128)} %bitcast.18, ...), custom_call_target="tpu_custom_call" | custom-call | tf_op jit(solution)/shard_map/kick/pallas_call | solution.py:834
  18.9 0.6 %copy.12 = f32[1,1,16,3,128]{4,2,3,1,0:T(8,128)} copy(f32[1,1,16,3,128]{4,2,3,1,0:T(8,128)S(1)} %bitcast.14) | data formatting | bytes 49152
